TPU v7x, 128 devices: a whole 4x4x4 slice. The times are simulated.
128 devices in a mesh: tp: 2 (over core), dp: 64 (over z, y, x).
Axes of the slice: x: 4, y: 4, z: 4, core: 2. Of those that a mesh axis runs over, the one named last changes fastest.
Arguments:
- token_ids: int32 [1024, 512], P('dp')
- embed_table: bfloat16 [50304, 512], P('tp')
- ln1_gain: bfloat16 [512], replicated
- ln1_bias: bfloat16 [512], replicated
- ln2_gain: bfloat16 [512], replicated
- ln2_bias: bfloat16 [512], replicated
- w_qkv: bfloat16 [512, 8, 3, 64], P(None, 'tp')
- b_qkv: bfloat16 [8, 3, 64], P('tp')
- w_dense: bfloat16 [8, 64, 512], P('tp')
- b_dense: bfloat16 [512], replicated
- w_fc1: bfloat16 [512, 2048], P(None, 'tp')
- b_fc1: bfloat16 [2048], P('tp')
- w_fc2: bfloat16 [2048, 512], P('tp')
- b_fc2: bfloat16 [512], replicated
- cotangent: bfloat16 [1024, 512, 512], P('dp')
Outputs:
- output 1: bfloat16 [1024, 512, 512], P('dp')
- output 2: float32 [50304, 512], P('tp', 'dp')
- output 3: float32 [512], P('dp')
- output 4: float32 [512], P('dp')
- output 5: float32 [512], P('dp')
- output 6: float32 [512], P('dp')
- output 7: float32 [512, 8, 3, 64], P('dp', 'tp')
- output 8: float32 [1536], P(('tp', 'dp'))
- output 9: float32 [8, 64, 512], P('tp', None, 'dp')
- output 10: float32 [512], P('dp')
- output 11: float32 [512, 2048], P('dp', 'tp')
- output 12: float32 [2048], P(('tp', 'dp'))
- output 13: float32 [2048, 512], P('tp', 'dp')
- output 14: float32 [512], P('dp')
All inputs are finite; a program needn't handle non-finite values.
Results may differ from a plain program's by a relative error of at most 0.00955545.
Values sent between devices are 32-bit elements.
A program may use at most 1 GiB of HBM per device.

v0:
```python
import functools
import jax
import jax.numpy as jnp
from jax import lax
from jax.sharding import PartitionSpec as P

EPS_NORM = 1e-5
ROPE_BASE = 10000.0
gelu_exact = functools.partial(jax.nn.gelu, approximate=False)


def rope_tables(seq_len, rot_dim):
    half_rot = rot_dim // 2
    inv_freq = ROPE_BASE ** (-(jnp.arange(half_rot, dtype=jnp.float32) * 2.0) / rot_dim)
    angles = jnp.arange(seq_len, dtype=jnp.float32)[:, None] * inv_freq[None, :]
    angles = jnp.concatenate([angles, angles], axis=-1)
    return jnp.cos(angles)[:, None, :], jnp.sin(angles)[:, None, :]


def apply_rope(tensor, cos_table, sin_table, rot_dim):
    half_rot = rot_dim // 2
    rot_part = tensor[..., :rot_dim]
    turned = jnp.concatenate([-rot_part[..., half_rot:], rot_part[..., :half_rot]], axis=-1)
    return jnp.concatenate([rot_part * cos_table + turned * sin_table, tensor[..., rot_dim:]], axis=-1)


def rope_back(grad_in, cos_table, sin_table, rot_dim):
    half_rot = rot_dim // 2
    rot_part = grad_in[..., :rot_dim]
    spun_part = rot_part * sin_table
    turned = jnp.concatenate([spun_part[..., half_rot:], -spun_part[..., :half_rot]], axis=-1)
    return jnp.concatenate([rot_part * cos_table + turned, grad_in[..., rot_dim:]], axis=-1)


def solution(mesh):
    arg_specs = (P('dp', None), P('tp', None), P(None), P(None), P(None), P(None), P(None, 'tp', None, None), P('tp', None, None), P('tp', None, None), P(None), P(None, 'tp'), P('tp'), P('tp', None), P(None), P('dp', None, None))
    out_specs = (P('dp', None, None), P('tp', 'dp'), P('dp'), P('dp'), P('dp'), P('dp'), P('dp', 'tp', None, None), P(('tp', 'dp')), P('tp', None, 'dp'), P('dp'), P('dp', 'tp'), P(('tp', 'dp')), P('tp', 'dp'), P('dp'))

    def device_step(token_ids, embed_table, ln1_gain, ln1_bias, ln2_gain, ln2_bias, w_qkv, b_qkv, w_dense, b_dense, w_fc1, b_fc1, w_fc2, b_fc2, cotangent):
        seq_len = token_ids.shape[1]
        vocab_local, d_model = embed_table.shape
        head_dim = w_qkv.shape[3]
        rot_dim = head_dim // 4
        attn_scale = head_dim ** -0.5
        local_ids = token_ids - lax.axis_index('tp') * vocab_local
        in_range = (local_ids >= 0) & (local_ids < vocab_local)
        picked = jnp.take(embed_table, jnp.where(in_range, local_ids, 0), axis=0)
        partial_x = jnp.where(in_range[..., None], picked, jnp.zeros_like(picked))
        x_float = lax.psum(partial_x.astype(jnp.float32), 'tp')
        mean_x = jnp.mean(x_float, axis=-1, keepdims=True)
        centered = x_float - mean_x
        inv_std = lax.rsqrt(jnp.mean(centered * centered, axis=-1, keepdims=True) + EPS_NORM)
        normed = centered * inv_std
        gain_attn = ln1_gain.astype(jnp.float32)
        gain_mlp = ln2_gain.astype(jnp.float32)
        hid_attn = (normed * gain_attn + ln1_bias.astype(jnp.float32)).astype(jnp.bfloat16)
        hid_mlp = (normed * gain_mlp + ln2_bias.astype(jnp.float32)).astype(jnp.bfloat16)
        qkv_all = (jnp.einsum('bsd,dhjc->bshjc', hid_attn, w_qkv, preferred_element_type=jnp.float32) + b_qkv.astype(jnp.float32)).astype(jnp.bfloat16)
        cos_table, sin_table = rope_tables(seq_len, rot_dim)
        queries = apply_rope(qkv_all[:, :, :, 0].astype(jnp.float32), cos_table, sin_table, rot_dim).astype(jnp.bfloat16)
        keys_rot = apply_rope(qkv_all[:, :, :, 1].astype(jnp.float32), cos_table, sin_table, rot_dim).astype(jnp.bfloat16)
        values = qkv_all[:, :, :, 2]
        causal = jnp.arange(seq_len)[:, None] >= jnp.arange(seq_len)[None, :]
        scores = jnp.einsum('bqhc,bkhc->bhqk', queries, keys_rot, preferred_element_type=jnp.float32) * attn_scale
        soft_probs = jax.nn.softmax(jnp.where(causal, scores, -1e30), axis=-1)
        probs_low = soft_probs.astype(jnp.bfloat16)
        context = jnp.einsum('bhqk,bkhc->bqhc', probs_low, values, preferred_element_type=jnp.float32).astype(jnp.bfloat16)
        pre_act = (jnp.einsum('bsd,df->bsf', hid_mlp, w_fc1, preferred_element_type=jnp.float32) + b_fc1.astype(jnp.float32)).astype(jnp.bfloat16)
        act_float, gelu_pull = jax.vjp(gelu_exact, pre_act.astype(jnp.float32))
        gelu_out = act_float.astype(jnp.bfloat16)
        partial_out = jnp.einsum('crid,ide->cre', context, w_dense, preferred_element_type=jnp.float32) + jnp.einsum('bsf,fd->bsd', gelu_out, w_fc2, preferred_element_type=jnp.float32)
        layer_sum = lax.psum(partial_out, 'tp')
        layer_out = (x_float + layer_sum + (b_dense.astype(jnp.float32) + b_fc2.astype(jnp.float32))).astype(jnp.bfloat16)

        cot_float = cotangent.astype(jnp.float32)
        bias_grad = jnp.sum(cot_float, axis=(0, 1))
        grad_act = jnp.einsum('bsd,fd->bsf', cotangent, w_fc2, preferred_element_type=jnp.float32).astype(jnp.bfloat16)
        (grad_pre_float,) = gelu_pull(grad_act.astype(jnp.float32))
        grad_pre = grad_pre_float.astype(jnp.bfloat16)
        part_wfc2 = jnp.einsum('bsf,bsd->fd', gelu_out, cotangent, preferred_element_type=jnp.float32)
        part_wfc1 = jnp.einsum('bsd,bsf->df', hid_mlp, grad_pre, preferred_element_type=jnp.float32)
        part_bfc1 = jnp.sum(grad_pre.astype(jnp.float32), axis=(0, 1))
        grad_hmlp = jnp.einsum('bsf,df->bsd', grad_pre, w_fc1, preferred_element_type=jnp.float32)
        part_wdense = jnp.einsum('crid,cre->ide', context, cotangent, preferred_element_type=jnp.float32)
        grad_ctx = jnp.einsum('cre,ide->crid', cotangent, w_dense, preferred_element_type=jnp.float32).astype(jnp.bfloat16)
        grad_probs = jnp.einsum('bqhc,bkhc->bhqk', grad_ctx, values, preferred_element_type=jnp.float32).astype(jnp.bfloat16).astype(jnp.float32)
        grad_values = jnp.einsum('bhqk,bqhc->bkhc', probs_low, grad_ctx, preferred_element_type=jnp.float32)
        grad_scores = (soft_probs * (grad_probs - jnp.sum(soft_probs * grad_probs, axis=-1, keepdims=True)) * attn_scale).astype(jnp.bfloat16)
        grad_queries = jnp.einsum('bhqk,bkhc->bqhc', grad_scores, keys_rot, preferred_element_type=jnp.float32).astype(jnp.bfloat16).astype(jnp.float32)
        grad_keys = jnp.einsum('bhqk,bqhc->bkhc', grad_scores, queries, preferred_element_type=jnp.float32).astype(jnp.bfloat16).astype(jnp.float32)
        grad_qkv = jnp.stack([rope_back(grad_queries, cos_table, sin_table, rot_dim), rope_back(grad_keys, cos_table, sin_table, rot_dim), grad_values], axis=3).astype(jnp.bfloat16)
        part_wqkv = jnp.einsum('bsd,bshjc->dhjc', hid_attn, grad_qkv, preferred_element_type=jnp.float32)
        part_bqkv = jnp.sum(grad_qkv.astype(jnp.float32), axis=(0, 1))
        grad_hattn = jnp.einsum('bshjc,dhjc->bsd', grad_qkv, w_qkv, preferred_element_type=jnp.float32)
        ln_parts = jnp.stack([jnp.sum(grad_hattn * normed, axis=(0, 1)), jnp.sum(grad_hattn, axis=(0, 1)), jnp.sum(grad_hmlp * normed, axis=(0, 1)), jnp.sum(grad_hmlp, axis=(0, 1))])
        grad_norm_part = grad_hattn * gain_attn + grad_hmlp * gain_mlp
        grad_norm = lax.psum(grad_norm_part, 'tp')
        grad_x = cot_float + inv_std * (grad_norm - jnp.mean(grad_norm, axis=-1, keepdims=True) - normed * jnp.mean(grad_norm * normed, axis=-1, keepdims=True))
        seg_ids = jnp.where(in_range, local_ids, vocab_local).reshape(-1)
        embed_part = jax.ops.segment_sum(grad_x.reshape(-1, d_model), seg_ids, num_segments=vocab_local, mode='drop')

        sum_embed = lax.psum_scatter(embed_part, 'dp', scatter_dimension=1, tiled=True)
        sum_ln = lax.psum(lax.psum_scatter(ln_parts, 'dp', scatter_dimension=1, tiled=True), 'tp')
        sum_wqkv = lax.psum_scatter(part_wqkv, 'dp', scatter_dimension=0, tiled=True)
        sum_bqkv = lax.psum_scatter(part_bqkv.reshape(-1), 'dp', scatter_dimension=0, tiled=True)
        sum_wdense = lax.psum_scatter(part_wdense, 'dp', scatter_dimension=2, tiled=True)
        sum_bias = lax.psum_scatter(bias_grad, 'dp', scatter_dimension=0, tiled=True)
        sum_wfc1 = lax.psum_scatter(part_wfc1, 'dp', scatter_dimension=0, tiled=True)
        sum_bfc1 = lax.psum_scatter(part_bfc1, 'dp', scatter_dimension=0, tiled=True)
        sum_wfc2 = lax.psum_scatter(part_wfc2, 'dp', scatter_dimension=1, tiled=True)
        return (layer_out, sum_embed, sum_ln[0], sum_ln[1], sum_ln[2], sum_ln[3], sum_wqkv, sum_bqkv, sum_wdense, sum_bias, sum_wfc1, sum_bfc1, sum_wfc2, sum_bias)

    return jax.shard_map(device_step, mesh=mesh, in_specs=arg_specs, out_specs=out_specs, check_vma=False)
```

profile of v0, /device:TPU:0, one launch (start us, length us, event | category | flops | bytes accessed | tf_op | source)
XLA Modules:
  0.0 2498.1 jit_solution(7675923535840288414)
XLA Ops:
  7.2 0.9 compare_and_fusion.1
  8.1 1.4 select_bitcast_fusion
  9.5 45.6 %gather_fusion = bf16[8192,512]{1,0:T(8,128)(2,1)} fusion(bf16[25152,512]{1,0:T(8,128)(2,1)} %param.16, s32[8192]{0:T(1024)S(1)} %broadcast_clamp_fusion), kind=kCustom, calls=%fused_computation | custom fusion | bytes 16809984 | tf_op jit(solution)/shard_map/jit(_take)/gather | solution.py:47
  55.1 9.8 select_convert_fusion
  65.2 0.5 convert_element_type.119
  65.7 0.6 convert_element_type.120
  66.3 0.6 copy.59
  67.0 0.7 fusion.111
  67.8 0.8 iota_compare_fusion
  68.5 7.8 fusion.73
  76.3 51.3 %all-reduce.11.cloned.1.call-done = f32[16,512,512]{2,1,0:T(8,128)} async-done(((f32[16,512,512]{2,1,0:T(8,128)}), f32[16,512,512]{2,1,0:T(8,128)}) %all-reduce.11.cloned.1.call-update) | async-done | bytes 16777232 | tf_op jit(solution)/shard_map/psum | solution.py:49
  127.6 6.9 reduce_sum.117
  134.6 7.4 multiply_reduce_fusion.2
  142.1 3.1 copy-done.1
  145.2 81.2 %fusion.37 = (f32[16,512,1024]{2,1,0:T(8,128)}, bf16[16,512,1024]{2,1,0:T(8,128)(2,1)}) fusion(f32[1024]{0:T(1024)S(1)} %convert_element_type.134, bf16[512,1024]{1,0:T(8,128)(2,1)S(1)} %copy-done, f32[512]{0:T(512)S(1)} %convert_element_type.132, f32[512]{0:T(512)S(1)} %convert_element_type.131, f32[16,512]{1,0:T(8,128)S(1)} %add_rsqrt_fusion, ...), kind=kOutput, calls=%fused_computation.48 | convolution fusion | flops 9156165632 | bytes 68231168 | tf_op jit(solution)/shard_map/bsd,df->bsf/dot_general | solution.py:68
  226.5 24.3 fusion.101
  250.8 31.2 %convert_reduce_fusion = (f32[1024]{0:T(1024)}, bf16[16,512,1024]{2,1,0:T(8,128)(2,1)}) fusion(f32[16,512,1024]{2,1,0:T(8,128)} %get-tuple-element.101, bf16[16,512,512]{2,1,0:T(8,128)(2,1)} %param.29, bf16[1024,512]{1,0:T(8,128)(2,1)S(1)} %copy-done.2, bf16[16,512,1024]{2,1,0:T(8,128)(2,1)} %get-tuple-element.102), kind=kOutput, calls=%fused_computation.56 | convolution fusion | flops 8749317120 | bytes 76550144 | tf_op jit(solution)/shard_map/bsd,fd->bsf/dot_general | solution.py:77
  282.0 14.1 add_convert_fusion.1
  296.2 9.4 fusion.126
  305.6 1.9 slice.120
  307.6 1.9 slice.115
  309.4 16.8 convolution_convert_fusion
  326.3 2.8 slice_negate_fusion.2
  329.1 3.4 fusion.88
  332.5 35.2 %fusion.132 = (f32[16,4,512]{2,1,0:T(4,128)}, f32[16,4,512,512]{2,3,1,0:T(8,128)}) fusion(pred[512,512]{0,1:T(8,128)(4,1)S(1)} %copy-done.13, bf16[16,512,4,48]{1,3,2,0:T(8,128)(2,1)} %slice.120, bf16[16,512,4,16]{1,3,2,0:T(8,128)(2,1)S(1)} %get-tuple-element.86, bf16[16,512,4,48]{1,3,2,0:T(8,128)(2,1)} %slice.115, ...), kind=kOutput, calls=%fused_computation.188 | convolution fusion | flops 2231370240 | bytes 75890688 | tf_op jit(solution)/shard_map/sub | solution.py:65
  367.8 25.4 %fusion.76 = bf16[16,4,64,512]{3,2,1,0:T(8,128)(2,1)} fusion(bf16[16,512,4,3,64]{1,4,3,2,0:T(8,128)(2,1)} %add_convert_fusion.1, f32[16,4,512,512]{2,3,1,0:T(8,128)} %get-tuple-element.104, f32[16,4,512]{2,1,0:T(4,128)} %get-tuple-element.103), kind=kOutput, calls=%fused_computation.113 | convolution fusion | flops 2183135232 | bytes 75628544 | tf_op jit(solution)/shard_map/bhqk,bkhc->bqhc/dot_general | solution.py:67
  393.2 65.8 %convert_bitcast_fusion.2 = bf16[16,512,4,64]{1,3,2,0:T(8,128)(2,1)} fusion(bf16[16,4,512,512]{2,3,1,0:T(8,128)(2,1)} %convolution_convert_fusion, bf16[16,512,4,48]{1,3,2,0:T(8,128)(2,1)} %slice.120, bf16[16,512,4,16]{1,3,2,0:T(8,128)(2,1)S(1)} %get-tuple-element.86, f32[16,4,512,512]{2,3,1,0:T(8,128)} %get-tuple-element.104, f32[16,4,512]{2,1,0:T(4,128)S(1)} %copy-done.38), kind=kOutput, calls=%fused_computation.111 | convolution fusion | flops 2308997632 | bytes 109182976 | tf_op jit(solution)/shard_map/bhqk,bkhc->bqhc/dot_general | solution.py:89
  459.0 79.7 %convert_bitcast_fusion.1 = bf16[16,512,4,64]{1,3,2,0:T(8,128)(2,1)} fusion(bf16[16,4,512,512]{2,3,1,0:T(8,128)(2,1)} %convolution_convert_fusion, bf16[16,512,4,48]{1,3,2,0:T(8,128)(2,1)} %slice.115, bf16[16,512,4,16]{1,3,2,0:T(8,128)(2,1)S(1)} %copy-done.4, f32[16,4,512,512]{2,3,1,0:T(8,128)} %get-tuple-element.104, f32[16,4,512]{2,1,0:T(4,128)S(1)} %copy-done.38), kind=kOutput, calls=%fused_computation.110 | convolution fusion | flops 2308997632 | bytes 109182976 | tf_op jit(solution)/shard_map/bhqk,bqhc->bkhc/dot_general | solution.py:90
  538.8 26.4 %convert_bitcast_fusion = bf16[16,512,4,1,64]{1,4,2,0,3:T(8,128)(2,1)} fusion(bf16[16,512,4,64]{1,3,2,0:T(8,128)(2,1)} %fusion.73, f32[16,4,512,512]{2,3,1,0:T(8,128)} %get-tuple-element.104, f32[16,4,512]{2,1,0:T(4,128)S(1)} %copy-done.38), kind=kOutput, calls=%fused_computation.109 | convolution fusion | flops 2183135232 | bytes 75628544 | tf_op jit(solution)/shard_map/bhqk,bqhc->bkhc/dot_general | solution.py:87
  565.1 4.0 slice.124
  569.1 4.3 convert_multiply_fusion.17
  573.4 16.3 fusion.103
  589.7 3.2 fusion.130
  593.0 3.2 fusion.131
  596.2 10.5 bitcast_add_fusion
  606.6 3.8 fusion.82
  610.4 2.2 maximum_bitcast_fusion
  612.7 0.4 maximum_bitcast_fusion.1
  613.1 11.6 convert_reduce_fusion.1
  624.8 17.3 fusion.52
  642.2 0.6 copy-done.14
  642.9 26.2 %fusion.89 = f32[512,4,3,64]{3,0,2,1:T(8,128)} fusion(bf16[16,512,4,3,64]{1,4,2,0,3:T(8,128)(2,1)} %get-tuple-element.69, f32[512]{0:T(512)S(1)} %copy-done.28, f32[512]{0:T(512)S(1)} %copy-done.26, f32[16,512]{1,0:T(8,128)S(1)} %copy-done.8, f32[16,512,512]{2,1,0:T(8,128)} %all-reduce.11.cloned.1.call-done, f32[16,512]{1,0:T(8,128)S(1)} %copy-done.6), kind=kOutput, calls=%fused_computation.130 | convolution fusion | flops 6463422464 | bytes 31002624 | tf_op jit(solution)/shard_map/bsd,bshjc->dhjc/dot_general | solution.py:92
  669.1 70.5 %all-reduce.15.cloned.1.call-done = (f32[16,512,512]{2,1,0:T(8,128)}, f32[16,512,512]{2,1,0:T(8,128)}) async-done(((f32[16,512,512]{2,1,0:T(8,128)}, f32[16,512,512]{2,1,0:T(8,128)}), (f32[16,512,512]{2,1,0:T(8,128)}, f32[16,512,512]{2,1,0:T(8,128)})) %all-reduce.15.cloned.1.call-update) | async-done | bytes 33554448 | tf_op jit(solution)/shard_map/psum | solution.py:72
  739.7 22.6 fusion.53
  762.3 29.2 %convert_add_fusion = (f32[16,512,512]{2,1,0:T(8,128)}, bf16[16,512,512]{2,1,0:T(8,128)(2,1)}, f32[512]{0:T(512)S(1)}) fusion(bf16[16,512,512]{2,1,0:T(8,128)(2,1)} %param.29, f32[16,512,512]{2,1,0:T(8,128)} %get-tuple-element.67, f32[16,512]{1,0:T(8,128)S(1)} %broadcast_multiply_fusion, f32[16,512]{1,0:T(8,128)S(1)} %broadcast_multiply_fusion.1, ...), kind=kLoop, calls=%fused_computation.69 | loop fusion | flops 50331136 | bytes 84021248 | tf_op jit(solution)/shard_map/add | solution.py:98
  791.6 69.6 %scatter_custom_fusion = f32[25152,512]{1,0:T(8,128)} fusion(s32[8192]{0:T(1024)S(1)} %bitcast.151, f32[8192,512]{1,0:T(8,128)} %bitcast.149, f32[]{:T(128)} %constant.52.clone.1), kind=kCustom, calls=%fused_computation.62 | custom fusion | flops 4194304 | bytes 51511808 | tf_op jit(solution)/shard_map/scatter-add | solution.py:100
  861.2 8.6 fusion.94
  869.9 22.5 convolution_bitcast_fusion
  892.6 16.0 convolution_bitcast_fusion.1
  908.6 0.6 dynamic-slice
  911.3 58.2 %reduce-scatter.7.cloned.1.call-done = f32[8,4,3,64]{3,0,2,1:T(8,128)} async-done(((f32[512,4,3,64]{3,0,2,1:T(8,128)}), f32[8,4,3,64]{3,0,2,1:T(8,128)}) %reduce-scatter.7.cloned.1.call-update) | async-done | bytes 24592 | tf_op jit(solution)/shard_map/reduce_scatter | solution.py:104
  969.4 1.4 copy.73
  970.9 348.7 %all-reduce.5 = (f32[4,512]{1,0:T(4,128)S(1)}, f32[768]{0:T(1024)S(1)}, f32[512]{0:T(512)S(1)}, f32[1024]{0:T(1024)S(1)}) all-reduce(f32[4,512]{1,0:T(4,128)S(1)} %pad_maximum_fusion.16, f32[768]{0:T(1024)S(1)} %reshape.121, f32[512]{0:T(512)S(1)} %get-tuple-element.76, ...), channel_id=3, replica_groups=mesh['tp'=2,'dp'=64] {'dp'}, use_global_device_ids=true, to_apply=%region_16.17.clone | all-reduce | flops 4352 | bytes 34816
  1319.7 0.6 dynamic-slice.9
  1320.3 0.6 dynamic-slice.5
  1320.9 2.4 psum.31
  1323.4 0.5 slice_bitcast_fusion.7
  1323.9 100.8 %all-reduce.13.cloned.1.call-done = f32[25152,512]{1,0:T(8,128)} async-done(((f32[25152,512]{1,0:T(8,128)}), f32[25152,512]{1,0:T(8,128)}) %all-reduce.13.cloned.1.call-update) | async-done | bytes 51511312
  1424.7 10.7 constant_dynamic-slice_fusion.1
  1435.4 8.2 copy.72
  1443.6 336.9 %reduce-scatter.9.cloned.1.call-done = f32[4,64,8]{1,2,0:T(8,128)} async-done(((f32[4,64,512]{1,2,0:T(8,128)}), f32[4,64,8]{1,2,0:T(8,128)}) %reduce-scatter.9.cloned.1.call-update) | async-done | bytes 8208 | tf_op jit(solution)/shard_map/reduce_scatter | solution.py:106
  1780.5 354.8 %reduce-scatter.13.cloned.1.call-done = f32[1024,8]{0,1:T(8,128)} async-done(((f32[1024,512]{0,1:T(8,128)}), f32[1024,8]{0,1:T(8,128)}) %reduce-scatter.13.cloned.1.call-update) | async-done | bytes 32784 | tf_op jit(solution)/shard_map/reduce_scatter | solution.py:110
  2135.3 355.0 %reduce-scatter.11.cloned.1.call-done = f32[8,1024]{1,0:T(8,128)} async-done(((f32[512,1024]{1,0:T(8,128)}), f32[8,1024]{1,0:T(8,128)}) %reduce-scatter.11.cloned.1.call-update) | async-done | bytes 32784 | tf_op jit(solution)/shard_map/reduce_scatter | solution.py:108
  2490.3 0.5 copy.113
  (128 shorter events, 1.2 us)
Async XLA Ops:
  7.2 134.9 %copy-start = (bf16[512,1024]{1,0:T(8,128)(2,1)S(1)}, bf16[512,1024]{1,0:T(8,128)(2,1)}, u32[]{:S(2)}) copy-start(bf16[512,1024]{1,0:T(8,128)(2,1)} %param.25) | copy-start | bytes 3145732
  7.2 120.4 %all-reduce.11.cloned.1.call-start = ((), (), s32[]{:S(2)}) async-start(), calls=%async_computation.4 | async-start | bytes 33554432 | tf_op jit(solution)/shard_map/psum | solution.py:49
  55.1 10.1 copy-start.29
  55.1 10.6 copy-start.30
  55.1 10.6 copy-start.31
  55.1 11.2 copy-start.32
  55.1 11.2 copy-start.19
  55.1 11.2 copy-start.18
  55.1 13.4 copy-start.12
  64.9 674.8 %all-reduce.15.cloned.1.call-start = ((), (), s32[]{:S(2)}) async-start(), calls=%async_computation.10 | async-start | bytes 67108864 | tf_op jit(solution)/shard_map/psum | solution.py:72
  65.7 76.3 %copy-start.20 = (f32[512]{0:T(512)}, f32[512]{0:T(512)S(1)}, u32[]{:S(2)}) copy-start(f32[512]{0:T(512)S(1)} %convert_element_type.131) | copy-start | bytes 6148
  66.3 75.7 %copy-start.23 = (f32[512]{0:T(512)}, f32[512]{0:T(512)S(1)}, u32[]{:S(2)}) copy-start(f32[512]{0:T(512)S(1)} %convert_element_type.132) | copy-start | bytes 6148
  134.6 10.6 copy-start.1
  134.6 147.4 %copy-start.5 = (f32[16,512]{1,0:T(8,128)}, f32[16,512]{1,0:T(8,128)S(1)}, u32[]{:S(2)}) copy-start(f32[16,512]{1,0:T(8,128)S(1)} %broadcast_multiply_fusion.2) | copy-start | bytes 98308
  145.2 136.8 %copy-start.7 = (f32[16,512]{1,0:T(8,128)}, f32[16,512]{1,0:T(8,128)S(1)}, u32[]{:S(2)}) copy-start(f32[16,512]{1,0:T(8,128)S(1)} %add_rsqrt_fusion) | copy-start | bytes 98308
  145.2 81.3 %copy-start.2 = (bf16[1024,512]{1,0:T(8,128)(2,1)S(1)}, bf16[1024,512]{1,0:T(8,128)(2,1)}, u32[]{:S(2)}) copy-start(bf16[1024,512]{1,0:T(8,128)(2,1)} %param.27) | copy-start | bytes 3145732
  250.8 31.2 %copy-start.16 = (f32[4,3,64]{2,1,0:T(4,128)S(1)}, f32[4,3,64]{2,1,0:T(4,128)}, u32[]{:S(2)}) copy-start(f32[4,3,64]{2,1,0:T(4,128)} %copy.59) | copy-start | bytes 9220
  250.8 31.2 %copy-start.25 = (f32[512]{0:T(512)S(1)}, f32[512]{0:T(512)}, u32[]{:S(2)}) copy-start(f32[512]{0:T(512)} %convert_element_type.119) | copy-start | bytes 6148
  250.8 31.3 %copy-start.27 = (f32[512]{0:T(512)S(1)}, f32[512]{0:T(512)}, u32[]{:S(2)}) copy-start(f32[512]{0:T(512)} %convert_element_type.120) | copy-start | bytes 6148
  250.8 31.3 %copy-start.35 = (bf16[512,4,3,64]{0,3,2,1:T(8,128)(2,1)S(1)}, bf16[512,4,3,64]{0,3,2,1:T(8,128)(2,1)}, u32[]{:S(2)}) copy-start(bf16[512,4,3,64]{0,3,2,1:T(8,128)(2,1)} %param.21) | copy-start | bytes 2359300
  309.4 19.6 copy-start.9
  309.4 19.6 copy-start.10
  326.3 6.3 copy-start.13
  332.5 35.3 %copy-start.3 = (bf16[16,512,4,16]{1,3,2,0:T(8,128)(2,1)}, bf16[16,512,4,16]{1,3,2,0:T(8,128)(2,1)S(1)}, u32[]{:S(2)}) copy-start(bf16[16,512,4,16]{1,3,2,0:T(8,128)(2,1)S(1)} %get-tuple-element.85) | copy-start | bytes 3145732
  367.8 25.4 %copy-start.38 = (f32[16,4,512]{2,1,0:T(4,128)S(1)}, f32[16,4,512]{2,1,0:T(4,128)}, u32[]{:S(2)}) copy-start(f32[16,4,512]{2,1,0:T(4,128)} %get-tuple-element.103) | copy-start | bytes 393220
  393.2 65.8 %copy-start.4 = (bf16[16,512,4,16]{1,3,2,0:T(8,128)(2,1)S(1)}, bf16[16,512,4,16]{1,3,2,0:T(8,128)(2,1)}, u32[]{:S(2)}) copy-start(bf16[16,512,4,16]{1,3,2,0:T(8,128)(2,1)} %copy-done.3) | copy-start | bytes 3145732
  538.7 30.4 %copy-start.11 = (f32[512,16]{0,1:T(8,128)S(1)}, f32[512,16]{0,1:T(8,128)}, u32[]{:S(2)}) copy-start(f32[512,16]{0,1:T(8,128)} %get-tuple-element.96) | copy-start | bytes 98308
  569.1 27.0 %slice-start = ((s8[16777216]{0:T(1024)(128)(4,1)}), s8[4194304]{0:T(1024)(128)(4,1)S(1)}, s32[]{:S(2)}) async-start(s8[16777216]{0:T(1024)(128)(4,1)} %bitcast.144), calls=%async_computation.11 | async-start | bytes 8388608
  573.4 22.7 slice-start.1
  573.4 22.7 slice-start.2
  573.4 22.7 slice-start.3
  606.6 6.0 slice-start.8
  612.6 12.1 slice-start.4
  612.6 12.1 copy-start.21
  612.7 12.1 copy-start.26
  613.1 11.6 slice-start.5
  613.1 11.6 slice-start.6
  613.1 11.6 slice-start.7
  642.1 0.8 copy-start.14
  642.1 0.8 copy-start.33
  642.1 0.8 copy-start.34
  642.1 0.8 copy-start.6
  642.1 0.8 copy-start.8
  642.1 0.8 copy-start.28
  642.1 327.3 %reduce-scatter.7.cloned.1.call-start = ((), (), s32[]{:S(2)}) async-start(), calls=%async_computation.5 | async-start | bytes 3194880 | tf_op jit(solution)/shard_map/reduce_scatter | solution.py:104
  669.1 755.6 %all-reduce.13.cloned.1.call-start = ((), (), s32[]{:S(2)}) async-start(), calls=%async_computation.9 | async-start | bytes 103022592
  861.2 919.3 %reduce-scatter.9.cloned.1.call-start = ((), (), s32[]{:S(2)}) async-start(), calls=%async_computation.6 | async-start | bytes 1064960 | tf_op jit(solution)/shard_map/reduce_scatter | solution.py:106
  869.8 22.7 copy-start.22
  869.8 22.7 copy-start.24
  869.9 1265.5 %reduce-scatter.13.cloned.1.call-start = ((), (), s32[]{:S(2)}) async-start(), calls=%async_computation.8 | async-start | bytes 2129920 | tf_op jit(solution)/shard_map/reduce_scatter | solution.py:110
  892.4 16.2 copy-start.36
  892.5 18.7 copy-start.15
  892.5 78.4 %copy-start.17 = (f32[1024]{0:T(1024)S(1)}, f32[1024]{0:T(1024)}, u32[]{:S(2)}) copy-start(f32[1024]{0:T(1024)} %get-tuple-element.107) | copy-start | bytes 12292
  892.5 1597.8 %reduce-scatter.11.cloned.1.call-start = ((), (), s32[]{:S(2)}) async-start(), calls=%async_computation.7 | async-start | bytes 2129920 | tf_op jit(solution)/shard_map/reduce_scatter | solution.py:108
  1319.7 1170.6 %copy-start.37 = (f32[8]{0:T(128)}, f32[8]{0:T(128)S(1)}, u32[]{:S(2)}) copy-start(f32[8]{0:T(128)S(1)} %dynamic-slice.7) | copy-start | bytes 100
Sparse Core Ops, SparseCore 0:
  65.0 62.5 all-reduce.10
  642.3 97.3 all-reduce.14
  744.1 225.3 reduce-scatter.6
  975.1 449.5 all-reduce.12
  1427.5 352.9 reduce-scatter.8
  1783.3 351.9 reduce-scatter.12
  2138.2 351.9 reduce-scatter.10
where the time goes:
time: 2500 us
  waiting for transfers between devices  1330 us (53%)
  matrix products  525 us (21%)
  blocking collectives  351 us (14%)
  other arithmetic  195 us (8%)
  local copies, waits for them, and re-layouts  81.4 us (3%)
    reduce_scatter x1, waiting for transfers between devices, device_step(): lax.psum_scatter(part_wfc1, 'dp', scatter_dimension=0, tiled=True)  355 us
    reduce_scatter x1, waiting for transfers between devices, device_step(): lax.psum_scatter(part_wfc2, 'dp', scatter_dimension=1, tiled=True)  355 us
    unnamed x1, blocking collectives  349 us
    reduce_scatter x1, waiting for transfers between devices, device_step(): lax.psum_scatter(part_wdense, 'dp', scatter_dimension=2, tiled=True)  337 us
    unnamed x8, waiting for transfers between devices  101 us
    dot_general x1, matrix products, device_step(): jnp.einsum('bsd,df->bsf', hid_mlp, w_fc1, preferred_element_type=jnp.floa...  81.2 us
    dot_general x1, matrix products, device_step(): jnp.einsum('bhqk,bqhc->bkhc', grad_scores, queries, preferred_element_typ...  79.7 us
    psum x1, waiting for transfers between devices, device_step(): layer_sum = lax.psum(partial_out, 'tp')  70.5 us
  transfers between devices with their start and end apart: 7, of which 7 were waited for; matrix products, arithmetic and copies ran while one was open for 9% of the time, Pallas kernels for 0%

commit v1 on v0

v1 whole, which is shorter than its diff:
```python
import functools
import math
import jax
import jax.numpy as jnp
from jax import lax
from jax.experimental import pallas as pl
from jax.experimental.pallas import tpu as pltpu
from jax.sharding import PartitionSpec as P

F32, BF16 = jnp.float32, jnp.bfloat16
NN = (((1,), (0,)), ((), ()))
NT = (((1,), (1,)), ((), ()))
TN = (((0,), (0,)), ((), ()))
S, D, FF, HEADS, HD = 512, 512, 2048, 8, 64
PAIR, HALF, PAIRS, FF_STEPS, ROT_HALF = 2 * HD, S // 2, HEADS // 2, FF // S, HD // 8
EPS, ROPE_BASE = 1e-5, 10000.0
LOG2E = 1.4426950408889634
SQRT_HALF, INV_SQRT_2PI = 0.7071067811865476, 0.3989422804014327
ERF_P = 0.35
ERF_C = (0.19746628636396, 0.19745311511580, 0.18590938935029, 0.15467161331132, 0.16294620242859,
         -0.014553608641014, 0.20121223107286, -0.085106053125625)
RB = 64
VMEM_LIMIT = 67_000_000
ROW, LANES, RING = 8, 128, 4
PAD = 25600
COLOR = PAD // 2
WIDE, EXTRA = 3072, 128
GCOLS = WIDE + EXTRA
MESH = pl.DeviceIdType.MESH
CHUNKS = (5, 3)


def dot(a, b, dims=NN):
    return lax.dot_general(a, b, dims, preferred_element_type=F32)


def rnd(v):
    return v.astype(BF16).astype(F32)


def gelu_parts(a):
    t = 1.0 / (1.0 + (ERF_P * SQRT_HALF) * jnp.abs(a))
    r = 0.5 * ERF_C[-1]
    for c in ERF_C[-2::-1]:
        r = r * t + 0.5 * c
    e = jnp.exp2(a * a * (-0.5 * LOG2E))
    q = r * t * e
    phi = jnp.where(a < 0, q, 1.0 - q)
    return a * phi, phi + a * e * INV_SQRT_2PI


def block(i, n):
    return slice(i * n, i * n + n)


def row_sums(v):
    return jnp.sum(v.reshape(RB // ROW, ROW, v.shape[-1]), axis=0)


def row_loop(body):
    @pl.loop(0, S // RB)
    def _(i):
        body(pl.ds(pl.multiple_of(i * RB, RB), RB))


def wcol(half, part, width):
    return slice(half * WIDE + part, half * WIDE + part + width)


def layer_kernel(carry, z_ref, xo_ref, xp_ref, cot_ref, vec_ref, bqkv_ref, bfc1_ref, rope_ref,
                 qo_ref, do_ref, fo_ref, to_ref, rp_ref, fp_ref, *refs):
    carried, refs = refs[:carry], refs[carry:]
    out_ref, gx_refs, (gw_ref, gs_ref, gb1_ref), refs = refs[0], refs[1:1 + RING], refs[1 + RING:RING + RING], refs[RING + RING:]
    (wqkv, wd, w1, w2, n_scr, inv_scr, x_scr, acc_scr, dh2_scr, a_scr, g_scr, h1_scr, h2_scr, h1t_scr, h2t_scr, cott_scr,
     dctx_scr, ctx_scr, u_scr, da_scr, qkv_scr, dqkv_scr) = refs

    @pl.when(pl.program_id(0) == 0)
    def _():
        if carried:
            for src, dst in zip(carried, (gw_ref, gs_ref, gb1_ref)):
                pltpu.sync_copy(src, dst)
        else:
            for dst in (gw_ref, gs_ref, gb1_ref):
                dst[...] = jnp.zeros_like(dst)
        for j in range(3):
            wqkv[block(2 * j, HALF), :] = qo_ref[block(j, HALF), :]
            wqkv[block(2 * j + 1, HALF), :] = rp_ref[block(j, HALF), :].astype(BF16)
        wd[:HALF, :] = do_ref[...]
        wd[HALF:, :] = rp_ref[block(3, HALF), :].astype(BF16)
        n = FF // 2
        w2[:n, :] = to_ref[...]
        w2[n:, :] = rp_ref[2 * S:, :].astype(BF16)
        w1[:, :n] = fo_ref[...]
        w1[:, n:] = fp_ref[...].astype(BF16)

    cot = cot_ref[0]
    g1, b1, g2, b2, bo = (vec_ref[i:i + 1, :] for i in range(5))

    def norm(rows):
        x = xo_ref[0, rows, :].astype(F32) + xp_ref[0, rows, :]
        x_scr[rows, :] = x
        cen = x - jnp.mean(x, axis=-1, keepdims=True)
        inv = lax.rsqrt(jnp.mean(cen * cen, axis=-1, keepdims=True) + EPS)
        n = cen * inv
        n_scr[rows, :] = n
        inv_scr[rows, :] = inv
        h1_scr[rows, :] = (n * g1 + b1).astype(BF16)
        h2_scr[rows, :] = (n * g2 + b2).astype(BF16)
        gs_ref[4] += row_sums(cot_ref[0, rows, :].astype(F32))
    row_loop(norm)

    h1t_scr[...] = h1_scr[...].T
    h2t_scr[...] = h2_scr[...].T
    cott_scr[...] = cot.T

    h1 = h1_scr[...]
    for p in range(PAIRS):
        for j in range(3):
            v = dot(h1, wqkv[block(j * PAIRS + p, PAIR), :], NT) + bqkv_ref[j:j + 1, block(p, PAIR)]
            v = v.astype(BF16)
            if j < 2:
                v = v.astype(F32)
                v = (v * rope_ref[0] + pltpu.roll(v, PAIR - ROT_HALF, 1) * rope_ref[1]
                     + pltpu.roll(v, ROT_HALF, 1) * rope_ref[2]).astype(BF16)
            qkv_scr[j, :, block(p, PAIR)] = v
    dctx_scr[...] = dot(cot, wd[...], NT).astype(BF16)

    lane = lax.broadcasted_iota(jnp.int32, (S, PAIR), 1)
    causal = lax.broadcasted_iota(jnp.int32, (HALF, HALF), 0) >= lax.broadcasted_iota(jnp.int32, (HALF, HALF), 1)
    zero = jnp.zeros((S, PAIR), BF16)

    def plus(lst, i, v):
        lst[i] = v if i not in lst else lst[i] + v

    for p in range(PAIRS):
        cs = block(p, PAIR)
        qp, kp, vp = (qkv_scr[j, :, cs] for j in range(3))
        dcp = dctx_scr[:, cs]
        ctx, dq, dk, dv = {}, {}, {}, {}
        for mine in (lane < HD, lane >= HD):
            qm, km, vm, dcm = (jnp.where(mine, w, zero) for w in (qp, kp, vp, dcp))
            for qb in range(2):
                kl = HALF * (qb + 1)
                qs = block(qb, HALF)
                s = dot(qm[qs], kp[:kl], NT)
                diag = jnp.where(causal, s[:, kl - HALF:], -1e30)
                s = jnp.concatenate([s[:, :HALF], diag], axis=1) if qb else diag
                e = jnp.exp2((s - jnp.max(s, axis=-1, keepdims=True)) * (HD ** -0.5 * LOG2E))
                pr = e * (1.0 / jnp.sum(e, axis=-1, keepdims=True))
                pb = pr.astype(BF16)
                plus(ctx, qb, dot(pb, vm[:kl]))
                dp = rnd(dot(dcm[qs], vp[:kl], NT))
                ds = (pr * (dp - jnp.sum(pr * dp, axis=-1, keepdims=True))).astype(BF16)
                plus(dq, qb, dot(ds, km[:kl]))
                dkb = dot(ds, qm[qs], TN)
                dvb = dot(pb, dcm[qs], TN)
                for kb in range(qb + 1):
                    plus(dk, kb, dkb[block(kb, HALF)])
                    plus(dv, kb, dvb[block(kb, HALF)])
        for b in range(2):
            bs = block(b, HALF)
            ctx_scr[bs, cs] = ctx[b].astype(BF16)
            for j, g in enumerate((dq[b], dk[b])):
                g = rnd(g * HD ** -0.5)
                spun = g * rope_ref[3, bs]
                dqkv_scr[j, bs, cs] = (g * rope_ref[0, bs] + pltpu.roll(spun, PAIR - ROT_HALF, 1) * rope_ref[4, bs]
                                       + pltpu.roll(spun, ROT_HALF, 1) * rope_ref[5, bs]).astype(BF16)
            dqkv_scr[2, bs, cs] = dv[b].astype(BF16)

    acc_scr[...] = dot(ctx_scr[...], wd[...])
    dh2_scr[...] = jnp.zeros_like(dh2_scr)
    h2 = h2_scr[...]
    for c in range(FF_STEPS):
        cs = block(c, S)
        a_scr[...] = dot(h2, w1[:, cs]) + bfc1_ref[:, cs]
        g_scr[...] = dot(cot, w2[cs, :], NT)

        def act(rows, cs=cs):
            u, gp = gelu_parts(rnd(a_scr[rows, :]))
            da = (rnd(g_scr[rows, :]) * gp).astype(BF16)
            u_scr[rows, :] = u.astype(BF16)
            da_scr[rows, :] = da
            gb1_ref[:, cs] += row_sums(da.astype(F32))
        row_loop(act)

        u, da = u_scr[...], da_scr[...]
        acc_scr[...] += dot(u, w2[cs, :])
        dh2_scr[...] += dot(da, w1[:, cs], NT)
        half, part = c // 2, 2 * S + c % 2 * S
        gw_ref[:, wcol(half, part, S)] += dot(h2t_scr[...], da)
        gw_ref[:, wcol(half, part + 2 * S, S)] += dot(cott_scr[...], u)

    for half in range(2):
        hs = block(half, HALF)
        for j in range(3):
            gw_ref[:, wcol(half, j * HALF, HALF)] += dot(h1t_scr[...], dqkv_scr[j, :, hs])
        gw_ref[:, wcol(half, 3 * HALF, HALF)] += dot(cott_scr[...], ctx_scr[:, hs])
    a_scr[...] = sum(dot(dqkv_scr[j], wqkv[block(j, S), :]) for j in range(3))
    z = z_ref[0]

    def back(rows):
        n = n_scr[rows, :]
        d1, d2 = rnd(a_scr[rows, :]), rnd(dh2_scr[rows, :])
        for i, v in zip((0, 1, 2, 3, 5, 6, 7), (d1 * n, d1, d2 * n, d2, *(dqkv_scr[j, rows, :].astype(F32) for j in range(3)))):
            gs_ref[i] += row_sums(v)
        gn = d1 * g1 + d2 * g2
        g_scr[rows, :] = cot_ref[0, rows, :].astype(F32) + inv_scr[rows, :] * (
            gn - jnp.mean(gn, axis=-1, keepdims=True) - n * jnp.mean(gn * n, axis=-1, keepdims=True))
        for k, ref in enumerate(gx_refs):
            ref[rows, :] = g_scr[rows, pl.ds(pl.multiple_of((z + k) % RING * LANES, LANES), LANES)]
        out_ref[0, rows, :] = rnd(x_scr[rows, :] + (acc_scr[rows, :] + bo))
    row_loop(back)


def rope_consts():
    inv_freq = ROPE_BASE ** (-jnp.arange(ROT_HALF, dtype=F32) / ROT_HALF)
    ang = jnp.arange(S, dtype=F32)[:, None] * inv_freq[None, :]
    cos, sin = jnp.cos(ang), jnp.sin(ang)
    one, zero = jnp.ones_like(cos), jnp.zeros_like(cos)
    keep, none = jnp.ones((S, HD - 2 * ROT_HALF), F32), jnp.zeros((S, HD - 2 * ROT_HALF), F32)
    parts = ((cos, cos, keep), (-sin, zero, none), (zero, sin, none), (sin, sin, none), (one, zero, none), (zero, -one, none))
    return jnp.stack([jnp.concatenate(p + p, axis=1) for p in parts])


def layer_call(first, count, carried, z, *args):
    vm, hbm = pl.BlockSpec(memory_space=pltpu.VMEM), pl.BlockSpec(memory_space=pl.ANY)
    seq = pl.BlockSpec((1, S, D), lambda i, _: (i + first, 0, 0))
    table, low = pltpu.VMEM((S, D), F32), pltpu.VMEM((S, D), BF16)
    return pl.pallas_call(
        functools.partial(layer_kernel, len(carried)),
        grid_spec=pltpu.PrefetchScalarGridSpec(
            num_scalar_prefetch=1, grid=(count,),
            in_specs=[seq] * 3 + [vm] * (len(args) - 3) + [hbm] * len(carried),
            out_specs=[pl.BlockSpec((1, S, D), lambda i, _: (i, 0, 0))] + [pl.BlockSpec((S, LANES), lambda i, _: (i, 0))] * RING + [vm] * 3,
            scratch_shapes=[pltpu.VMEM((3 * S, D), BF16), low, pltpu.VMEM((D, FF), BF16), pltpu.VMEM((FF, D), BF16), table,
                            pltpu.VMEM((S, 1), F32)] + [table] * 5 + [low] * 9 + [pltpu.VMEM((3, S, D), BF16)] * 2),
        out_shape=[jax.ShapeDtypeStruct((count, S, D), F32)] + [jax.ShapeDtypeStruct((count * S, LANES), F32)] * RING
        + [jax.ShapeDtypeStruct((D, 2 * WIDE), F32), jax.ShapeDtypeStruct((ROW, ROW, D), F32), jax.ShapeDtypeStruct((ROW, FF), F32)],
        compiler_params=pltpu.CompilerParams(dimension_semantics=("arbitrary",), vmem_limit_bytes=VMEM_LIMIT),
        cost_estimate=pl.CostEstimate(flops=count * 30_000_000_000, bytes_accessed=60_000_000, transcendentals=0),
        name="layer",
    )(z, *args, *carried)


def merge_kernel(firsts, half, core_ref, *refs):
    i = pl.program_id(0)
    for src, (own, first, count) in zip(refs[:-1], firsts):
        at = i - first - half * jnp.where(own, core_ref[0], 1 - core_ref[0])

        @pl.when((at >= 0) & (at < count))
        def _():
            refs[-1][...] = src[...].astype(BF16)


def merge_call(core, owns, others):
    counts = [v.shape[0] for v in owns]
    half = sum(counts)
    firsts = [(own, sum(counts[:j]), n) for own in (True, False) for j, n in enumerate(counts)]

    def spec(own, first, count):
        return pl.BlockSpec((1, S, D), lambda i, c: (
            jnp.clip(i - first - half * (c[0] if own else 1 - c[0]), 0, count - 1), 0, 0))
    return pl.pallas_call(
        functools.partial(merge_kernel, firsts, half),
        grid_spec=pltpu.PrefetchScalarGridSpec(
            num_scalar_prefetch=1, grid=(2 * half,), in_specs=[spec(*f) for f in firsts],
            out_specs=pl.BlockSpec((1, S, D), lambda i, c: (i, 0, 0))),
        out_shape=jax.ShapeDtypeStruct((2 * half, S, D), BF16),
        name="merge",
    )(core.reshape(1).astype(jnp.int32), *owns, *others)


STEPS, UNROLL = 8, 8
STEP = PAD // STEPS


def table_kernel(half, ids_ref, *refs):
    rows, (out_ref, acc, acc2, stage, sem) = refs[:-5], refs[-5:]

    @pl.loop(0, acc.shape[0] // LANES)
    def _(j):
        for a in (acc, acc2):
            a[pl.ds(pl.multiple_of(j * LANES, LANES), LANES), :] = jnp.zeros((LANES, LANES), F32)
    start = 0
    for even, odd in zip(rows[::2], rows[1::2]):
        count = even.shape[0]

        @pl.loop(0, count // UNROLL)
        def _(g, start=start, count=count, even=even, odd=odd):
            t0 = pl.multiple_of(g * UNROLL, UNROLL)
            for j in range(UNROLL):
                for a, src, base in ((acc, even, start), (acc2, odd, start + count)):
                    row = pl.ds(ids_ref[base + t0 + j], 1)
                    a[row, :] += src[pl.ds(t0 + j, 1), :]
        start += 2 * count
    copies = []
    for i in range(2 * STEPS):
        h, c, slot = i // STEPS, i % STEPS, i % 2
        if i > 1:
            copies[i - 2].wait()

        @pl.loop(0, STEP // LANES, unroll=5)
        def _(b):
            at = pl.ds(pl.multiple_of(h * half + c * STEP + b * LANES, ROW), LANES)
            stage[slot, :, pl.ds(pl.multiple_of(b * LANES, LANES), LANES)] = (acc[at, :] + acc2[at, :]).T
        copies.append(pltpu.make_async_copy(stage.at[slot], out_ref.at[h, :, pl.ds(c * STEP, STEP)], sem.at[slot]))
        copies[i].start()
    for c in copies[-2:]:
        c.wait()


def table_call(ids, rows, half):
    return pl.pallas_call(
        functools.partial(table_kernel, half),
        grid_spec=pltpu.PrefetchScalarGridSpec(
            num_scalar_prefetch=1, grid=(), in_specs=[pl.BlockSpec(memory_space=pltpu.VMEM)] * len(rows),
            out_specs=pl.BlockSpec(memory_space=pl.ANY),
            scratch_shapes=[pltpu.VMEM((half + PAD, LANES), F32)] * 2 + [pltpu.VMEM((2, LANES, STEP), F32), pltpu.SemaphoreType.DMA((2,))]),
        out_shape=jax.ShapeDtypeStruct((2, LANES, PAD), F32),
        compiler_params=pltpu.CompilerParams(vmem_limit_bytes=VMEM_LIMIT),
        cost_estimate=pl.CostEstimate(flops=4_000_000_000, bytes_accessed=34_000_000, transcendentals=0),
        name="table",
    )(ids, *rows)


def cut(lo, n):
    first = n // (2 * LANES) * LANES
    return (lo, first), (lo + first, n - first)


def over(lead, body, at=()):
    if not lead:
        return body(at)

    @pl.loop(0, lead[0])
    def _(i):
        over(lead[1:], body, at + (i,))


def add_into(dst, srcs, lead, lo, n):
    def body(at):
        v = dst[at + (slice(None), pl.ds(lo, n))]
        for s in srcs:
            v = v + s[at + (slice(None), pl.ds(0, n))]
        dst[at + (slice(None), pl.ds(lo, n))] = v
    over(lead, body)


def tail_kernel(t_ref, g_ref, e_ref, oute_ref, outw_ref, *scratch):
    tsum, tpeer, gsum, gpeer, send, recv, local = scratch[:7]
    bufs = list(scratch[7:])
    core, dp = lax.axis_index('tp'), lax.axis_index('dp')
    pos = {'z': dp // (RING * RING), 'y': dp // RING % RING, 'x': dp % RING}
    stride = {'z': RING * RING, 'y': RING, 'x': 1}

    def shift(axis, k):
        return (pos[axis] + k) % RING

    def device(axis, k):
        return (core, dp + (shift(axis, k) - pos[axis]) * stride[axis])
    peer = (1 - core, dp)

    barrier = pltpu.get_barrier_semaphore()
    near = [peer] + [device(axis, k) for axis in 'zyx' for k in (1, RING - 1)]
    for who in near:
        pl.semaphore_signal(barrier, inc=1, device_id=who, device_id_type=MESH)
    pl.semaphore_wait(barrier, len(near))

    used = [0, 0]

    def remote(src, dst, who):
        i = used[0]
        used[0] += 1
        c = pltpu.make_async_remote_copy(src, dst, send.at[i], recv.at[i], device_id=who, device_id_type=MESH)
        c.start()
        return c

    def load(src, dst):
        i = used[1]
        used[1] += 1
        c = pltpu.make_async_copy(src, dst, local.at[i])
        c.start()
        return c
    sent = []

    full = pl.ds(0, COLOR)
    rest = pl.ds(COLOR, COLOR)
    wide, extra, far = pl.ds(0, WIDE), pl.ds(WIDE, EXTRA), pl.ds(WIDE, WIDE)
    every = slice(None)
    views = {
        'a': ('y', lambda i: (i, every, every, full)),
        'b': ('x', lambda i: (every, i, every, rest)),
        'g': ('z', lambda i: (i, every, every, every, wide)),
    }
    pend = {}
    pend['e'] = [remote(e_ref.at[1], gpeer.at[every, every, every, every, extra], peer),
                 load(e_ref.at[0], gsum.at[every, every, every, every, extra])]
    for k in (2, 1, RING - 1, 0):
        for name, (axis, view) in views.items():
            at = view(shift(axis, k))
            if name == 'g':
                there = at[:-1] + (far,)
                pend[name, k] = [remote(g_ref.at[there], gpeer.at[at], peer), load(g_ref.at[at], gsum.at[at])]
            else:
                pend[name, k] = [remote(t_ref.at[(1,) + at], tpeer.at[at], peer), load(t_ref.at[(0,) + at], tsum.at[at])]

    def arrive(key):
        out, here = pend[key]
        sent.append(out)
        out.wait_recv()
        here.wait()

    def ready(name, k):
        arrive((name, k))
        axis, _ = views[name]
        i = shift(axis, k)
        if name == 'a':
            add_into(tsum.at[i], [tpeer.at[i]], (RING,), 0, COLOR)
        elif name == 'b':
            add_into(tsum.at[:, i, :, rest], [tpeer.at[:, i, :, rest]], (RING,), 0, COLOR)
        else:
            add_into(gsum.at[i], [gpeer.at[i]], (RING, RING), 0, GCOLS)

    class Stage:
        def __init__(self, axis, piece, lead, lo, n, need=None):
            self.axis, self.piece, self.lead, self.lo, self.n, self.need = axis, piece, lead, lo, n, need
            self.halves = cut(lo, n)
            self.near = [bufs.pop(0), bufs.pop(0)]
            self.last = [bufs.pop(0), bufs.pop(0)]

        def view(self, k, lo, n):
            return self.piece(shift(self.axis, k)).at[(every,) * (len(self.lead) + 1) + (pl.ds(lo, n),)]

        def want(self, k):
            if self.need:
                ready(self.need, k)

        def first(self):
            self.want(2)
            self.c1 = [remote(self.view(2, *self.halves[s]), self.near[s], device(self.axis, k))
                       for s, k in enumerate((1, RING - 1))]

        def second(self):
            self.want(1)
            self.want(RING - 1)
            self.c2 = []
            for s, k in enumerate((1, RING - 1)):
                self.c1[s].wait_recv()
                add_into(self.piece(shift(self.axis, k)), [self.near[s]], self.lead, *self.halves[s])
                self.c2.append(remote(self.view(k, self.lo, self.n), self.last[s], device(self.axis, k)))

        def finish(self):
            self.want(0)
            for c in self.c2:
                c.wait_recv()
            add_into(self.piece(shift(self.axis, 0)), self.last, self.lead, self.lo, self.n)
            sent.extend(self.c1 + self.c2)

    py, px, pz = pos['y'], pos['x'], pos['z']
    one, two = (RING,), (RING, RING)
    a1 = Stage('y', lambda i: tsum.at[i], one, 0, COLOR, 'a')
    b1 = Stage('x', lambda i: tsum.at[:, i], one, COLOR, COLOR, 'b')
    g1 = Stage('z', lambda i: gsum.at[i], two, 0, GCOLS, 'g')
    a2 = Stage('x', lambda i: tsum.at[py, i], (), 0, COLOR)
    b2 = Stage('y', lambda i: tsum.at[i, px], (), COLOR, COLOR)
    (c0, cn), (d0, dn) = cut(0, GCOLS)
    c1 = Stage('y', lambda i: gsum.at[pz, i], one, c0, cn)
    d1 = Stage('x', lambda i: gsum.at[pz, :, i], one, d0, dn)
    c2 = Stage('x', lambda i: gsum.at[pz, py, i], (), c0, cn)
    d2 = Stage('y', lambda i: gsum.at[pz, i, px], (), d0, dn)

    a1.first()
    b1.first()
    arrive('e')
    g1.first()
    for phase in ('second', 'finish'):
        for s in (a1, b1, g1):
            getattr(s, phase)()
            if phase == 'finish':
                for t in {a1: (a2,), b1: (b2,), g1: (c1, d1)}[s]:
                    t.first()
    for s in (a2, b2, c1, d1):
        s.second()
    for s in (a2, b2):
        s.finish()
    oute_ref[...] = tsum[py, px, :, 0:oute_ref.shape[1]]
    for s, t in ((c1, c2), (d1, d2)):
        s.finish()
        t.first()
    for s in (c2, d2):
        s.second()
    for s in (c2, d2):
        s.finish()
    outw_ref[...] = gsum[pz, py, px]
    for c in sent:
        c.wait_send()


def tail_call(t, g, e, rows):
    def ring_bufs(lead, n):
        (_, p), (_, q) = cut(0, n)
        return [pltpu.VMEM(lead + (ROW, w), F32) for w in (p, q, n, n)]
    (_, cn), (_, dn) = cut(0, GCOLS)
    one, two, three = (RING,), (RING,) * 2, (RING,) * 3
    bufs = sum((ring_bufs(*b) for b in ((one, COLOR), (one, COLOR), (two, GCOLS), ((), COLOR), ((), COLOR),
                                        (one, cn), (one, dn), ((), cn), ((), dn))), [])
    dma = pltpu.SemaphoreType.DMA
    hbm = pl.BlockSpec(memory_space=pl.ANY)
    vm = pl.BlockSpec(memory_space=pltpu.VMEM)
    return pl.pallas_call(
        tail_kernel,
        in_specs=[hbm] * 3, out_specs=[vm] * 2,
        out_shape=[jax.ShapeDtypeStruct((ROW, rows), F32), jax.ShapeDtypeStruct((ROW, GCOLS), F32)],
        scratch_shapes=[pltpu.VMEM(two + (ROW, PAD), F32)] * 2 + [pltpu.VMEM(three + (ROW, GCOLS), F32)] * 2
        + [dma((64,)), dma((64,)), dma((16,))] + bufs,
        compiler_params=pltpu.CompilerParams(collective_id=0, has_side_effects=True, vmem_limit_bytes=VMEM_LIMIT),
        name="tail",
    )(t, g, e)


def solution(mesh):
    tp, dp, no = 'tp', 'dp', None
    one, vec_dp, both = P(no), P(dp), P((tp, dp))
    arg_specs = (P(dp, no), P(tp, no), one, one, one, one, P(no, tp, no, no), P(tp, no, no), P(tp, no, no), one, P(no, tp), P(tp), P(tp, no), one, P(dp, no, no))
    out_specs = (P(dp, no, no), P(tp, dp), vec_dp, vec_dp, vec_dp, vec_dp, P(dp, tp, no, no), both, P(tp, no, dp), vec_dp, P(dp, tp), both, P(tp, dp), vec_dp)
    chips = mesh.shape[dp]
    plane = chips // RING

    def swap(v):
        return lax.ppermute(v, tp, [(0, 1), (1, 0)])

    def z_shift(v, k):
        return lax.ppermute(v, dp, [(i, (i + k * plane) % chips) for i in range(chips)]) if k else v

    def device_step(token_ids, embed_table, ln1_gain, ln1_bias, ln2_gain, ln2_bias, w_qkv, b_qkv, w_dense, b_dense, w_fc1, b_fc1, w_fc2, b_fc2, cotangent):
        core = lax.axis_index(tp)
        z = (lax.axis_index(dp) // plane).reshape(1)
        vocab_local = embed_table.shape[0]
        seqs = token_ids.shape[0] // 2
        f = lambda v: v.astype(F32)

        wq_own = w_qkv.transpose(2, 1, 3, 0).reshape(3 * HALF, D)
        wd_own = w_dense.reshape(HALF, D)
        rows_peer = swap(f(jnp.concatenate([wq_own, wd_own, w_fc2], axis=0)))
        fc1_peer = swap(f(w_fc1))
        b_peer = swap(f(jnp.concatenate([b_qkv.reshape(-1), b_fc1])))
        bqkv = jnp.concatenate([f(b_qkv), b_peer[:b_qkv.size].reshape(b_qkv.shape)], axis=0).transpose(1, 0, 2).reshape(3, D)
        bfc1 = jnp.concatenate([f(b_fc1), b_peer[b_qkv.size:]]).reshape(1, FF)
        vec = jnp.stack([f(ln1_gain), f(ln1_bias), f(ln2_gain), f(ln2_bias), f(b_dense) + f(b_fc2)])

        def lookup(ids):
            local = ids - core * vocab_local
            ok = (local >= 0) & (local < vocab_local)
            got = jnp.take(embed_table, jnp.where(ok, local, 0), axis=0)
            return jnp.where(ok[..., None], got, jnp.zeros_like(got))

        ids_own = lax.dynamic_slice_in_dim(token_ids, core * seqs, seqs, 0)
        ids_peer = lax.dynamic_slice_in_dim(token_ids, (1 - core) * seqs, seqs, 0)
        cot = lax.dynamic_slice_in_dim(cotangent, core * seqs, seqs, 0)
        x_peer = swap(f(lookup(ids_peer)))
        x_own = lookup(ids_own)
        flat = ids_own.reshape(-1)
        ids_z = [z_shift(flat, k) for k in range(RING)]

        args = (x_own, x_peer, cot, vec, bqkv, bfc1, rope_consts(), wq_own, wd_own, w_fc1, w_fc2, rows_peer, fc1_peer)
        carried, owns, others, rows, row_ids, first = (), [], [], [], [], 0
        for count in CHUNKS:
            out, *gx_carried = layer_call(first, count, carried, z, *args)
            gx, carried = gx_carried[:RING], gx_carried[RING:]
            owns.append(out)
            others.append(swap(out))
            rows += [z_shift(gx[k], k) for k in range(RING)]
            row_ids += [ids_z[k][first * S:(first + count) * S] for k in range(RING)]
            first += count
        grad_w, grad_s, grad_b1 = carried
        layer_out = merge_call(core, owns, others)

        ids = jnp.concatenate(row_ids) - core * vocab_local
        dense = table_call(jnp.where(ids < 0, ids + 2 * vocab_local, ids), rows, vocab_local)

        small = jnp.sum(grad_s, axis=1)
        norms = small[:5].reshape(5, chips, ROW).transpose(1, 0, 2).reshape(chips, 5 * ROW)
        grad_bq = small[5:].reshape(3, 2, PAIRS, HD).transpose(1, 2, 0, 3).reshape(2, chips, -1)
        grad_bf = jnp.sum(grad_b1, axis=0).reshape(2, chips, -1)
        extra = jnp.concatenate([jnp.stack([norms, norms]), grad_bq, grad_bf], axis=2)
        ends = (5 * ROW, 5 * ROW + grad_bq.shape[2], extra.shape[2])
        extra = jnp.pad(extra[:, :, None, :], ((0, 0), (0, 0), (0, ROW - 1), (0, EXTRA - ends[2])))
        ring3 = (RING,) * 3
        sum_embed, total = tail_call(dense.reshape(2, RING, RING, ROW, PAD), grad_w.reshape(ring3 + (ROW, 2 * WIDE)),
                                     extra.reshape((2,) + ring3 + (ROW, EXTRA)), vocab_local)
        qkv, wide = 3 * HALF, 4 * HALF
        sum_wqkv = total[:, :qkv].reshape(ROW, 3, PAIRS, HD).transpose(0, 2, 1, 3)
        sum_wdense = total[:, qkv:wide].reshape(ROW, PAIRS, HD).transpose(1, 2, 0)
        sum_wfc1, sum_wfc2 = total[:, wide:2 * wide], total[:, 2 * wide:WIDE].T
        last = total[0, WIDE:]
        n1g, n1b, n2g, n2b, bias = last[:ends[0]].reshape(5, ROW)
        return (layer_out, sum_embed.T, n1g, n1b, n2g, n2b, sum_wqkv, last[ends[0]:ends[1]], sum_wdense, bias, sum_wfc1,
                last[ends[1]:ends[2]], sum_wfc2, bias)

    return jax.shard_map(device_step, mesh=mesh, in_specs=arg_specs, out_specs=out_specs, check_vma=False)
```

time: 2500 us -> 689 us (0.28)
  waiting for transfers between devices: 1330 us -> 77.7 us
  matrix products: 525 us -> 0 us
  Pallas kernels: 0 us -> 471 us
  blocking collectives: 351 us -> 0 us
  other arithmetic: 195 us -> 20 us
    reduce_scatter x4 -> x0, waiting for transfers between devices: 1100 us -> none  [the longest x1 355 us: device_step(): lax.psum_scatter(part_wfc1, 'dp', scatter_dimension=0, tiled=True)]
    dot_general x17 -> x0, matrix products: 490 us -> none  [the longest x1 81.2 us: device_step(): jnp.einsum('bsd,df->bsf', hid_mlp, w_fc1, preferred_element_type=jnp.floa...]
    pallas_call x0 -> x5, Pallas kernels: none -> 471 us  [the longest x2 296 us: layer_call(): pl.pallas_call(functools.partial(layer_kernel, len(carried)), grid_spec=p...]
    unnamed x1 -> x0, blocking collectives: 349 us -> none
    psum x2 -> x0, waiting for transfers between devices: 122 us -> none  [the longest x1 70.5 us: device_step(): layer_sum = lax.psum(partial_out, 'tp')]
    unnamed x8 -> x0, waiting for transfers between devices: 101 us -> none
    ppermute x0 -> x15, waiting for transfers between devices: none -> 77.7 us  [the longest x9 77.6 us: z_shift(): lax.ppermute(v, dp, [(i, (i + k * plane) % chips) for i in range(chips)])]
    scatter-add x1 -> x0, other arithmetic: 69.6 us -> none  [device_step(): jax.ops.segment_sum(grad_x.reshape(-1, d_model), seg_ids, num_segments=vo...]
  transfers between devices with their start and end apart: 7 -> 15, of which waited for: 7 -> 5; matrix products, arithmetic and copies ran while one was open for 9% -> 11% of each run, Pallas kernels for 0% -> 67%
where the time goes in v1:
time: 689 us; the launch traced here: 682 us
  Pallas kernels  471 us (68%)
  local copies, waits for them, and re-layouts  99.2 us (14%)
  waiting for transfers between devices  77.7 us (11%)
  other arithmetic  20 us (3%)
  starting transfers between devices  13.4 us (2%)
    pallas_call x2, Pallas kernels, layer_call(): pl.pallas_call(functools.partial(layer_kernel, len(carried)), grid_spec=p...  296 us
    pallas_call x1, Pallas kernels, tail_call(): pl.pallas_call(tail_kernel, in_specs=[hbm] * 3, out_specs=[vm] * 2, out_s...  99.9 us
    ppermute x9, waiting for transfers between devices, z_shift(): lax.ppermute(v, dp, [(i, (i + k * plane) % chips) for i in range(chips)])  77.6 us
    pallas_call x1, Pallas kernels, table_call(): pl.pallas_call(functools.partial(table_kernel, half), grid_spec=pltpu.Pre...  59.2 us
    gather x2, local copies, waits for them, and re-layouts, lookup(): got = jnp.take(embed_table, jnp.where(ok, local, 0), axis=0)  58.2 us
    unnamed x59, local copies, waits for them, and re-layouts  18.5 us
    pallas_call x1, Pallas kernels, merge_call(): pl.pallas_call(functools.partial(merge_kernel, firsts, half), grid_spec=p...  15 us
  transfers between devices with their start and end apart: 15, of which 5 were waited for; matrix products, arithmetic and copies ran while one was open for 11% of the time, Pallas kernels for 67%

profile of v1, /device:TPU:0, one launch (start us, length us, event | category | flops | bytes accessed | tf_op | source)
XLA Modules:
  0.0 682.2 jit_solution(2013482550316318630)
XLA Ops:
  0.7 0.8 compare_and_fusion
  1.4 0.8 dynamic-slice_bitcast_fusion
  2.2 29.1 %gather_fusion.1 = bf16[4096,512]{1,0:T(8,128)(2,1)} fusion(bf16[25152,512]{1,0:T(8,128)(2,1)} %param.18, s32[4096]{0:T(1024)S(1)} %get-tuple-element.70), kind=kCustom, calls=%fused_computation.1.clone | custom fusion | bytes 8404992 | tf_op jit(solution)/shard_map/jit(_take)/gather | solution.py:554
  31.3 7.1 %fusion = f32[8,512,512]{2,1,0:T(8,128)} fusion(bf16[8,512,512]{2,1,0:T(8,128)(2,1)} %bitcast.64, pred[8,512]{1,0:T(8,128)(4,1)S(1)} %get-tuple-element.51, pred[8,512]{1,0:T(8,128)(4,1)S(1)} %get-tuple-element.52), kind=kLoop, calls=%fused_computation.3 | loop fusion | flops 6291456 | bytes 12591104 | tf_op jit(solution)/shard_map/convert_element_type | solution.py:540
  38.5 0.9 copy-done.1
  39.4 2.6 maximum_convert_fusion
  42.9 0.6 collective-permute-start.3
  43.5 0.6 copy.53
  44.1 2.2 collective-permute-start.6
  46.3 29.2 %gather_fusion = bf16[4096,512]{1,0:T(8,128)(2,1)} fusion(bf16[25152,512]{1,0:T(8,128)(2,1)} %param.18, s32[4096]{0:T(1024)S(1)} %get-tuple-element.71), kind=kCustom, calls=%fused_computation.clone | custom fusion | bytes 8404992 | tf_op jit(solution)/shard_map/jit(_take)/gather | solution.py:554
  75.5 1.0 fusion.1
  76.5 1.1 concatenate.36
  77.7 1.1 concatenate.35
  78.8 1.1 concatenate.34
  80.4 1.0 bitcast_dynamic-update-slice_fusion.2
  81.4 1.2 copy-done.10
  82.6 1.7 bitcast_dynamic-update-slice_fusion.1
  84.3 0.7 bitcast_dynamic-update-slice_fusion
  85.0 1.7 constant_dynamic-update-slice_fusion.1
  86.7 0.7 constant_dynamic-update-slice_fusion.rope_ref
  87.4 4.6 constant_dynamic-slice_fusion.2.cot_ref
  92.1 3.7 select_select_fusion.1.xo_ref
  95.7 1.3 constant_dynamic-update-slice_fusion.2
  97.2 0.6 stack.57.vec_ref
  97.8 3.6 collective-permute-start.7
  101.5 0.7 reshape.116.bqkv_ref
  102.2 0.6 pad_maximum_fusion
  102.8 1.0 collective-permute-start.8
  103.8 184.2 %layer.2 = (f32[5,512,512]{2,1,0:T(8,128)}, f32[2560,128]{1,0:T(8,128)}, f32[2560,128]{1,0:T(8,128)}, f32[2560,128]{1,0:T(8,128)}, f32[2560,128]{1,0:T(8,128)}, ...) custom-call(s32[1]{0:T(128)} %bitcast.1.z_ref, bf16[8,512,512]{2,1,0:T(8,128)(2,1)} %select_select_fusion.1.xo_ref, ...), custom_call_target="tpu_custom_call" | custom-call | flops 149999992832 | bytes 60000000 | tf_op jit(solution)/shard_map/layer/pallas_call | solution.py:229
  288.0 112.3 %layer.3 = (f32[3,512,512]{2,1,0:T(8,128)}, f32[1536,128]{1,0:T(8,128)}, f32[1536,128]{1,0:T(8,128)}, f32[1536,128]{1,0:T(8,128)}, f32[1536,128]{1,0:T(8,128)}, ...) custom-call(s32[1]{0:T(128)} %bitcast.1.z_ref, bf16[8,512,512]{2,1,0:T(8,128)(2,1)} %select_select_fusion.1.xo_ref, ...), custom_call_target="tpu_custom_call" | custom-call | flops 89999998976 | bytes 60000000 | tf_op jit(solution)/shard_map/layer/pallas_call | solution.py:229
  400.4 1.1 collective-permute-start.12
  401.5 0.5 collective-permute-start.13
  402.0 2.2 collective-permute-start.14
  404.2 0.7 constant_dynamic-slice_fusion
  405.1 1.3 slice_dynamic-update-slice_fusion.2
  406.4 1.3 slice_dynamic-update-slice_fusion.1
  407.7 1.3 slice_dynamic-update-slice_fusion
  409.1 29.4 %collective-permute-done.12.refs_5_ = f32[1536,128]{1,0:T(8,128)} collective-permute-done((f32[1536,128]{1,0:T(8,128)}, f32[1536,128]{1,0:T(8,128)}, u32[]{:S(2)}, u32[]{:S(2)}) %collective-permute-start.12) | collective-permute-done | bytes 786464 | tf_op jit(solution)/shard_map/ppermute | solution.py:533
  438.4 0.7 collective-permute-done.14.refs_7_
  439.1 1.3 collective-permute-start.9
  440.5 1.3 constant_dynamic-update-slice_fusion.3
  441.8 1.3 slice_dynamic-update-slice_fusion.5
  443.1 1.3 slice_dynamic-update-slice_fusion.4
  444.4 1.3 slice_dynamic-update-slice_fusion.3
  445.7 1.5 compare_select_fusion.ids_ref
  447.2 0.9 reduce_sum.18
  448.7 0.9 reduce_sum.19
  449.8 0.8 pad.4.clone
  450.6 21.1 %collective-permute-done.10.refs_2_ = f32[2560,128]{1,0:T(8,128)} collective-permute-done((f32[2560,128]{1,0:T(8,128)}, f32[2560,128]{1,0:T(8,128)}, u32[]{:S(2)}, u32[]{:S(2)}) %collective-permute-start.10) | collective-permute-done | bytes 1310752 | tf_op jit(solution)/shard_map/ppermute | solution.py:533
  471.7 23.6 %collective-permute-done.11.refs_3_ = f32[2560,128]{1,0:T(8,128)} collective-permute-done((f32[2560,128]{1,0:T(8,128)}, f32[2560,128]{1,0:T(8,128)}, u32[]{:S(2)}, u32[]{:S(2)}) %collective-permute-start.11) | collective-permute-done | bytes 1310752 | tf_op jit(solution)/shard_map/ppermute | solution.py:533
  495.3 2.9 collective-permute-done.9.refs_1_
  498.2 59.2 %table.1 = f32[2,128,25600]{2,1,0:T(8,128)} custom-call(s32[16384]{0:T(1024)} %compare_select_fusion.ids_ref, f32[2560,128]{1,0:T(8,128)} %get-tuple-element.38.refs_0_, f32[2560,128]{1,0:T(8,128)} %collective-permute-done.9.refs_1_, f32[2560,128]{1,0:T(8,128)} %collective-permute-done.10.refs_2_, f32[2560,128]{1,0:T(8,128)} %collective-permute-done.11.refs_3_, ...), custom_call_target="tpu_custom_call" | custom-call | flops 4000000000 | bytes 34000000 | tf_op jit(solution)/shard_map/table/pallas_call | solution.py:313
  557.5 99.9 %tail.1 = (f32[8,25152]{1,0:T(8,128)}, f32[8,3200]{1,0:T(8,128)}) custom-call(f32[2,4,4,8,25600]{4,3,2,1,0:T(8,128)} %bitcast.62, f32[4,4,4,8,6144]{4,3,2,1,0:T(8,128)} %bitcast.65, f32[2,4,4,4,8,128]{5,4,3,2,1,0:T(8,128)} %bitcast.69), custom_call_target="tpu_custom_call" | custom-call | tf_op jit(solution)/shard_map/tail/pallas_call | solution.py:510
  657.4 0.7 slice.96
  658.1 0.7 slice.99
  658.8 0.7 reshape.128
  659.6 0.6 copy.55
  660.2 1.5 slice_bitcast_fusion.2
  661.6 1.3 slice_bitcast_fusion.1
  662.9 1.3 slice_bitcast_fusion.3
  664.2 1.4 slice_bitcast_fusion
  665.6 15.0 %merge.1 = bf16[16,512,512]{2,1,0:T(8,128)(2,1)} custom-call(s32[1]{0:T(128)} %bitcast.core_ref, f32[5,512,512]{2,1,0:T(8,128)} %get-tuple-element.33.refs_0_, f32[3,512,512]{2,1,0:T(8,128)} %get-tuple-element.37.refs_1_, f32[5,512,512]{2,1,0:T(8,128)} %collective-permute-done.4.refs_2_, f32[3,512,512]{2,1,0:T(8,128)} %collective-permute-done.5.refs_3_), custom_call_target="tpu_custom_call" | custom-call | tf_op jit(solution)/shard_map/merge/pallas_call | solution.py:263
  680.6 0.5 copy.71
  681.1 0.9 copy.72
  (97 shorter events, 2.8 us)
Async XLA Ops:
  31.3 7.2 %copy-start.6 = (bf16[512,4,3,64]{0,3,2,1:T(8,128)(2,1)S(1)}, bf16[512,4,3,64]{0,3,2,1:T(8,128)(2,1)}, u32[]{:S(2)}) copy-start(bf16[512,4,3,64]{0,3,2,1:T(8,128)(2,1)} %param.23) | copy-start | bytes 2359300
  31.3 8.1 %copy-start.4 = (bf16[1024,512]{1,0:T(8,128)(2,1)S(1)}, bf16[1024,512]{1,0:T(8,128)(2,1)}, u32[]{:S(2)}) copy-start(bf16[1024,512]{1,0:T(8,128)(2,1)} %to_ref.3) | copy-start | bytes 3145732
  31.3 8.1 %copy-start.7 = (bf16[4,64,512]{2,1,0:T(8,128)(2,1)S(1)}, bf16[4,64,512]{2,1,0:T(8,128)(2,1)}, u32[]{:S(2)}) copy-start(bf16[4,64,512]{2,1,0:T(8,128)(2,1)} %param.25) | copy-start | bytes 786436
  38.4 4.1 copy-start.11
  38.4 4.2 copy-start.12
  38.4 4.3 copy-start.2
  38.4 65.4 %collective-permute-start = (f32[8,512,512]{2,1,0:T(8,128)}, f32[8,512,512]{2,1,0:T(8,128)}, u32[]{:S(2)}, u32[]{:S(2)}) collective-permute-start(f32[8,512,512]{2,1,0:T(8,128)} %fusion), channel_id=1, source_target_pairs={{0,64},{64,0},{1,65},{65,1},{2,66},{66,2},{3,67},{67,3},{4,68},{68... | collective-permute-start | bytes 25165832 | tf_op jit(solution)/shard_map/ppermute | solution.py:530
  38.5 0.9 copy-start.1
  42.0 61.8 %collective-permute-start.2 = (f32[2048,512]{1,0:T(8,128)}, f32[2048,512]{1,0:T(8,128)}, u32[]{:S(2)}, u32[]{:S(2)}) collective-permute-start(f32[2048,512]{1,0:T(8,128)} %maximum_convert_fusion), channel_id=1, source_target_pairs={{0,64},{64,0},{1,65},{65,1},{2,66},{66,2},{3,67},{67,3},{4,68},{68... | collective-permute-start | bytes 12582920 | tf_op jit(solution)/shard_map/ppermute | solution.py:530
  42.6 55.2 %collective-permute-start.1 = (f32[1792]{0:T(1024)S(1)}, f32[1792]{0:T(1024)S(1)}, u32[]{:S(2)}, u32[]{:S(2)}) collective-permute-start(f32[1792]{0:T(1024)S(1)} %maximum_convert_fusion.1), channel_id=1, source_target_pairs={{0,64},{64,0},{1,65},{65,1},{2,66},{66,2},{3,67},{67,3},{4,68},{68... | collective-permute-start | bytes 21512 | tf_op jit(solution)/shard_map/ppermute | solution.py:530
  42.9 59.8 %collective-permute-start.3 = (f32[512,1024]{1,0:T(8,128)S(1)}, f32[512,1024]{1,0:T(8,128)}, u32[]{:S(2)}, u32[]{:S(2)}) collective-permute-start(f32[512,1024]{1,0:T(8,128)S(1)} %convert_element_type.37), channel_id=1, source_target_pairs={{0,64},{64,0},{1,65},{65,1},{2,66},{66,2},{3,67},{67,3},{4,68},{68... | collective-permute-start | bytes 6291464 | tf_op jit(solution)/shard_map/ppermute | solution.py:530
  44.1 357.4 %collective-permute-start.6 = (s32[4096]{0:T(1024)}, s32[4096]{0:T(1024)}, u32[]{:S(2)}, u32[]{:S(2)}) collective-permute-start(s32[4096]{0:T(1024)} %bitcast.41), channel_id=1, source_target_pairs={{0,16},{1,17},{2,18},{3,19},{4,20},{5,21},{6,22},{7,23},{8,24},{9,... | collective-permute-start | bytes 49160 | tf_op jit(solution)/shard_map/ppermute | solution.py:533
  76.5 6.0 copy-start.9
  78.8 5.4 copy-start.3
  79.9 6.7 copy-start.8
  81.4 1.2 copy-start.10
  87.4 4.6 copy-start.17
  87.4 4.6 copy-start.18
  87.4 4.6 copy-start
  92.0 5.1 copy-start.13
  92.0 5.1 copy-start.14
  92.0 5.1 copy-start.15
  92.0 5.1 copy-start.16
  97.8 304.2 %collective-permute-start.7 = (s32[4096]{0:T(1024)}, s32[4096]{0:T(1024)}, u32[]{:S(2)}, u32[]{:S(2)}) collective-permute-start(s32[4096]{0:T(1024)} %bitcast.41), channel_id=1, source_target_pairs={{0,32},{1,33},{2,34},{3,35},{4,36},{5,37},{6,38},{7,39},{8,40},{9,... | collective-permute-start | bytes 49160 | tf_op jit(solution)/shard_map/ppermute | solution.py:533
  102.8 302.2 %collective-permute-start.8 = (s32[4096]{0:T(1024)}, s32[4096]{0:T(1024)}, u32[]{:S(2)}, u32[]{:S(2)}) collective-permute-start(s32[4096]{0:T(1024)} %bitcast.41), channel_id=1, source_target_pairs={{0,48},{1,49},{2,50},{3,51},{4,52},{5,53},{6,54},{7,55},{8,56},{9,... | collective-permute-start | bytes 49160 | tf_op jit(solution)/shard_map/ppermute | solution.py:533
  287.9 377.6 %collective-permute-start.4 = (f32[5,512,512]{2,1,0:T(8,128)}, f32[5,512,512]{2,1,0:T(8,128)}, u32[]{:S(2)}, u32[]{:S(2)}) collective-permute-start(f32[5,512,512]{2,1,0:T(8,128)} %get-tuple-element.33.refs_0_), channel_id=1, source_target_pairs={{0,64},{64,0},{1,65},{65,1},{2,66},{66,2},{3,67},{67,3},{4,68},{68... | collective-permute-start | bytes 15728648 | tf_op jit(solution)/shard_map/ppermute | solution.py:530
  400.4 38.0 %collective-permute-start.12 = (f32[1536,128]{1,0:T(8,128)}, f32[1536,128]{1,0:T(8,128)}, u32[]{:S(2)}, u32[]{:S(2)}) collective-permute-start(f32[1536,128]{1,0:T(8,128)} %get-tuple-element.43), channel_id=1, source_target_pairs={{0,16},{1,17},{2,18},{3,19},{4,20},{5,21},{6,22},{7,23},{8,24},{9,... | collective-permute-start | bytes 2359304 | tf_op jit(solution)/shard_map/ppermute | solution.py:533
  401.5 37.0 %collective-permute-start.13 = (f32[1536,128]{1,0:T(8,128)}, f32[1536,128]{1,0:T(8,128)}, u32[]{:S(2)}, u32[]{:S(2)}) collective-permute-start(f32[1536,128]{1,0:T(8,128)} %get-tuple-element.44), channel_id=1, source_target_pairs={{0,32},{1,33},{2,34},{3,35},{4,36},{5,37},{6,38},{7,39},{8,40},{9,... | collective-permute-start | bytes 2359304 | tf_op jit(solution)/shard_map/ppermute | solution.py:533
  402.0 37.1 %collective-permute-start.14 = (f32[1536,128]{1,0:T(8,128)}, f32[1536,128]{1,0:T(8,128)}, u32[]{:S(2)}, u32[]{:S(2)}) collective-permute-start(f32[1536,128]{1,0:T(8,128)} %get-tuple-element.45), channel_id=1, source_target_pairs={{0,48},{1,49},{2,50},{3,51},{4,52},{5,53},{6,54},{7,55},{8,56},{9,... | collective-permute-start | bytes 2359304 | tf_op jit(solution)/shard_map/ppermute | solution.py:533
  405.0 260.6 %collective-permute-start.5 = (f32[3,512,512]{2,1,0:T(8,128)}, f32[3,512,512]{2,1,0:T(8,128)}, u32[]{:S(2)}, u32[]{:S(2)}) collective-permute-start(f32[3,512,512]{2,1,0:T(8,128)} %get-tuple-element.37.refs_1_), channel_id=1, source_target_pairs={{0,64},{64,0},{1,65},{65,1},{2,66},{66,2},{3,67},{67,3},{4,68},{68... | collective-permute-start | bytes 9437192 | tf_op jit(solution)/shard_map/ppermute | solution.py:530
  438.4 33.3 %collective-permute-start.10 = (f32[2560,128]{1,0:T(8,128)}, f32[2560,128]{1,0:T(8,128)}, u32[]{:S(2)}, u32[]{:S(2)}) collective-permute-start(f32[2560,128]{1,0:T(8,128)} %get-tuple-element.40), channel_id=1, source_target_pairs={{0,32},{1,33},{2,34},{3,35},{4,36},{5,37},{6,38},{7,39},{8,40},{9,... | collective-permute-start | bytes 3932168 | tf_op jit(solution)/shard_map/ppermute | solution.py:533
  438.4 56.9 %collective-permute-start.11 = (f32[2560,128]{1,0:T(8,128)}, f32[2560,128]{1,0:T(8,128)}, u32[]{:S(2)}, u32[]{:S(2)}) collective-permute-start(f32[2560,128]{1,0:T(8,128)} %get-tuple-element.41), channel_id=1, source_target_pairs={{0,48},{1,49},{2,50},{3,51},{4,52},{5,53},{6,54},{7,55},{8,56},{9,... | collective-permute-start | bytes 3932168 | tf_op jit(solution)/shard_map/ppermute | solution.py:533
  439.1 59.1 %collective-permute-start.9 = (f32[2560,128]{1,0:T(8,128)}, f32[2560,128]{1,0:T(8,128)}, u32[]{:S(2)}, u32[]{:S(2)}) collective-permute-start(f32[2560,128]{1,0:T(8,128)} %get-tuple-element.39), channel_id=1, source_target_pairs={{0,16},{1,17},{2,18},{3,19},{4,20},{5,21},{6,22},{7,23},{8,24},{9,... | collective-permute-start | bytes 3932168 | tf_op jit(solution)/shard_map/ppermute | solution.py:533
  661.6 18.9 %copy-start.19 = (f32[8]{0:T(128)}, f32[8]{0:T(128)S(1)}, u32[]{:S(2)}) copy-start(f32[8]{0:T(128)S(1)} %get-tuple-element.123) | copy-start | bytes 100
  665.6 15.5 %copy-start.5 = (f32[8,25152]{1,0:T(8,128)S(1)}, f32[8,25152]{1,0:T(8,128)}, u32[]{:S(2)}) copy-start(f32[8,25152]{1,0:T(8,128)} %get-tuple-element.49) | copy-start | bytes 2414596

commit v2 on v1

--- a/solution.py
+++ b/solution.py
@@ -19,7 +19,7 @@
 ERF_P = 0.35
 ERF_C = (0.19746628636396, 0.19745311511580, 0.18590938935029, 0.15467161331132, 0.16294620242859,
          -0.014553608641014, 0.20121223107286, -0.085106053125625)
-RB = 64
+RB = 128
 VMEM_LIMIT = 67_000_000
 ROW, LANES, RING = 8, 128, 4
 PAD = 25600
@@ -27,7 +27,6 @@
 WIDE, EXTRA = 3072, 128
 GCOLS = WIDE + EXTRA
 MESH = pl.DeviceIdType.MESH
-CHUNKS = (5, 3)
 
 
 def dot(a, b, dims=NN):
@@ -67,31 +66,82 @@
     return slice(half * WIDE + part, half * WIDE + part + width)
 
 
-def layer_kernel(carry, z_ref, xo_ref, xp_ref, cot_ref, vec_ref, bqkv_ref, bfc1_ref, rope_ref,
-                 qo_ref, do_ref, fo_ref, to_ref, rp_ref, fp_ref, *refs):
-    carried, refs = refs[:carry], refs[carry:]
-    out_ref, gx_refs, (gw_ref, gs_ref, gb1_ref), refs = refs[0], refs[1:1 + RING], refs[1 + RING:RING + RING], refs[RING + RING:]
-    (wqkv, wd, w1, w2, n_scr, inv_scr, x_scr, acc_scr, dh2_scr, a_scr, g_scr, h1_scr, h2_scr, h1t_scr, h2t_scr, cott_scr,
-     dctx_scr, ctx_scr, u_scr, da_scr, qkv_scr, dqkv_scr) = refs
-
-    @pl.when(pl.program_id(0) == 0)
+def layer_kernel(xo_ref, xp_ref, cot_ref, vec_ref, bqkv_ref, bfc1_ref, rope_ref, qo_ref, do_ref, fo_ref, to_ref, rp_ref, fp_ref,
+                 out_ref, rows_ref, gw_ref, gs_ref, gb1_ref,
+                 wqkv, wd, w1, w2, n_scr, inv_scr, x_scr, acc_scr, dh2_scr, a_scr, g_scr, h1_scr, h2_scr, h1t_scr, h2t_scr, cott_scr,
+                 dctx_scr, ctx_scr, u_scr, da_scr, qkv_scr, dqkv_scr,
+                 gx_buf, out_buf, peer_buf, own_low, peer_low, gx_send, gx_recv, gx_local, out_send, out_recv, own_sem, peer_sem, init_sem):
+    step, last = pl.program_id(0), pl.num_programs(0) - 1
+    slot = step % 2
+    core, chip = lax.axis_index('tp'), lax.axis_index('dp')
+    chips = lax.axis_size('dp')
+    plane = chips // RING
+    z, peer = chip // plane, (1 - core, chip)
+
+    def z_device(k):
+        return (core, (chip + k * plane) % chips)
+
+    @pl.when(step == 0)
     def _():
-        if carried:
-            for src, dst in zip(carried, (gw_ref, gs_ref, gb1_ref)):
-                pltpu.sync_copy(src, dst)
-        else:
-            for dst in (gw_ref, gs_ref, gb1_ref):
-                dst[...] = jnp.zeros_like(dst)
+        barrier = pltpu.get_barrier_semaphore()
+        near = [peer] + [z_device(k) for k in range(1, RING)]
+        for who in near:
+            pl.semaphore_signal(barrier, inc=1, device_id=who, device_id_type=MESH)
+        pl.semaphore_wait(barrier, len(near))
+        for dst in (gw_ref, gs_ref, gb1_ref):
+            dst[...] = jnp.zeros_like(dst)
+        n = FF // 2
+        moves = [(qo_ref.at[block(j, HALF)], wqkv.at[block(2 * j, HALF)]) for j in range(3)]
+        moves += [(do_ref, wd.at[:HALF]), (to_ref, w2.at[:n]), (fo_ref, w1.at[:, :n])]
+        tables = (n_scr, x_scr, acc_scr, dh2_scr, a_scr, g_scr)
+        parts = [rp_ref.at[block(i, S)] for i in range(RING)] + [fp_ref.at[:, block(i, S)] for i in range(2)]
+        copies = [pltpu.make_async_copy(src, dst, init_sem.at[i]) for i, (src, dst) in enumerate(moves + list(zip(parts, tables)))]
+        for c in copies:
+            c.start()
+        for c in copies:
+            c.wait()
         for j in range(3):
-            wqkv[block(2 * j, HALF), :] = qo_ref[block(j, HALF), :]
-            wqkv[block(2 * j + 1, HALF), :] = rp_ref[block(j, HALF), :].astype(BF16)
-        wd[:HALF, :] = do_ref[...]
-        wd[HALF:, :] = rp_ref[block(3, HALF), :].astype(BF16)
-        n = FF // 2
-        w2[:n, :] = to_ref[...]
-        w2[n:, :] = rp_ref[2 * S:, :].astype(BF16)
-        w1[:, :n] = fo_ref[...]
-        w1[:, n:] = fp_ref[...].astype(BF16)
+            wqkv[block(2 * j + 1, HALF), :] = tables[j // 2][block(j % 2, HALF), :].astype(BF16)
+        wd[HALF:, :] = tables[1][HALF:, :].astype(BF16)
+        for i in range(2):
+            w2[block(2 + i, S), :] = tables[2 + i][...].astype(BF16)
+            w1[:, block(2 + i, S)] = tables[RING + i][...].astype(BF16)
+
+    def gx_copy(at, k):
+        rows = pl.ds(pl.multiple_of(at * S, S), S)
+        src, dst = gx_buf.at[at % 2, k], rows_ref.at[k, rows]
+        if k:
+            return pltpu.make_async_remote_copy(src, dst, gx_send.at[at % 2, k], gx_recv.at[at, k], device_id=z_device(k), device_id_type=MESH)
+        return pltpu.make_async_copy(src, dst, gx_local.at[at % 2])
+
+    def out_copy(at):
+        return pltpu.make_async_remote_copy(out_buf.at[at % 2], peer_buf.at[at], out_send.at[at % 2], out_recv.at[at], device_id=peer, device_id_type=MESH)
+
+    def own_store(at):
+        return pltpu.make_async_copy(own_low.at[at % 2], out_ref.at[core * (last + 1) + at], own_sem.at[at % 2])
+
+    def peer_store(at):
+        return pltpu.make_async_copy(peer_low.at[at % 2], out_ref.at[(1 - core) * (last + 1) + at], peer_sem.at[at % 2])
+
+    def drain(at):
+        gx_copy(at, 0).wait()
+        for k in range(1, RING):
+            gx_copy(at, k).wait_send()
+        out_copy(at).wait_send()
+        own_store(at).wait()
+
+    def take_peer(at):
+        out_copy(at).wait_recv()
+
+        @pl.when(at > 1)
+        def _():
+            peer_store(at - 2).wait()
+        peer_low[at % 2] = peer_buf[at].astype(BF16)
+        peer_store(at).start()
+
+    @pl.when(step > 1)
+    def _():
+        drain(step - 2)
 
     cot = cot_ref[0]
     g1, b1, g2, b2, bo = (vec_ref[i:i + 1, :] for i in range(5))
@@ -196,7 +246,6 @@
             gw_ref[:, wcol(half, j * HALF, HALF)] += dot(h1t_scr[...], dqkv_scr[j, :, hs])
         gw_ref[:, wcol(half, 3 * HALF, HALF)] += dot(cott_scr[...], ctx_scr[:, hs])
     a_scr[...] = sum(dot(dqkv_scr[j], wqkv[block(j, S), :]) for j in range(3))
-    z = z_ref[0]
 
     def back(rows):
         n = n_scr[rows, :]
@@ -206,10 +255,32 @@
         gn = d1 * g1 + d2 * g2
         g_scr[rows, :] = cot_ref[0, rows, :].astype(F32) + inv_scr[rows, :] * (
             gn - jnp.mean(gn, axis=-1, keepdims=True) - n * jnp.mean(gn * n, axis=-1, keepdims=True))
-        for k, ref in enumerate(gx_refs):
-            ref[rows, :] = g_scr[rows, pl.ds(pl.multiple_of((z + k) % RING * LANES, LANES), LANES)]
-        out_ref[0, rows, :] = rnd(x_scr[rows, :] + (acc_scr[rows, :] + bo))
+        for k in range(RING):
+            gx_buf[slot, k, rows, :] = g_scr[rows, pl.ds(pl.multiple_of((z + k) % RING * LANES, LANES), LANES)]
+        low = (x_scr[rows, :] + (acc_scr[rows, :] + bo)).astype(BF16)
+        own_low[slot, rows, :] = low
+        out_buf[slot, rows, :] = low.astype(F32)
     row_loop(back)
+    for k in range(RING):
+        gx_copy(step, k).start()
+    out_copy(step).start()
+    own_store(step).start()
+
+    @pl.when(step > 0)
+    def _():
+        take_peer(step - 1)
+
+    @pl.when(step == last)
+    def _():
+        take_peer(step)
+        for at in (step - 1, step):
+            drain(at)
+            peer_store(at).wait()
+
+        @pl.loop(0, last + 1)
+        def _(at):
+            for k in range(1, RING):
+                gx_copy(at, k).wait_recv()
 
 
 def rope_consts():
@@ -222,77 +293,48 @@
     return jnp.stack([jnp.concatenate(p + p, axis=1) for p in parts])
 
 
-def layer_call(first, count, carried, z, *args):
+def layer_call(*args):
+    count = args[0].shape[0]
     vm, hbm = pl.BlockSpec(memory_space=pltpu.VMEM), pl.BlockSpec(memory_space=pl.ANY)
-    seq = pl.BlockSpec((1, S, D), lambda i, _: (i + first, 0, 0))
-    table, low = pltpu.VMEM((S, D), F32), pltpu.VMEM((S, D), BF16)
+    seq = pl.BlockSpec((1, S, D), lambda i: (i, 0, 0))
+    table, low, dma = pltpu.VMEM((S, D), F32), pltpu.VMEM((S, D), BF16), pltpu.SemaphoreType.DMA
     return pl.pallas_call(
-        functools.partial(layer_kernel, len(carried)),
-        grid_spec=pltpu.PrefetchScalarGridSpec(
-            num_scalar_prefetch=1, grid=(count,),
-            in_specs=[seq] * 3 + [vm] * (len(args) - 3) + [hbm] * len(carried),
-            out_specs=[pl.BlockSpec((1, S, D), lambda i, _: (i, 0, 0))] + [pl.BlockSpec((S, LANES), lambda i, _: (i, 0))] * RING + [vm] * 3,
-            scratch_shapes=[pltpu.VMEM((3 * S, D), BF16), low, pltpu.VMEM((D, FF), BF16), pltpu.VMEM((FF, D), BF16), table,
-                            pltpu.VMEM((S, 1), F32)] + [table] * 5 + [low] * 9 + [pltpu.VMEM((3, S, D), BF16)] * 2),
-        out_shape=[jax.ShapeDtypeStruct((count, S, D), F32)] + [jax.ShapeDtypeStruct((count * S, LANES), F32)] * RING
-        + [jax.ShapeDtypeStruct((D, 2 * WIDE), F32), jax.ShapeDtypeStruct((ROW, ROW, D), F32), jax.ShapeDtypeStruct((ROW, FF), F32)],
-        compiler_params=pltpu.CompilerParams(dimension_semantics=("arbitrary",), vmem_limit_bytes=VMEM_LIMIT),
+        layer_kernel,
+        grid=(count,),
+        in_specs=[seq] * 3 + [vm] * 4 + [hbm] * (len(args) - 7),
+        out_specs=[hbm] * 2 + [vm] * 3,
+        out_shape=[jax.ShapeDtypeStruct((2 * count, S, D), BF16), jax.ShapeDtypeStruct((RING, count * S, LANES), F32),
+                   jax.ShapeDtypeStruct((D, 2 * WIDE), F32), jax.ShapeDtypeStruct((ROW, ROW, D), F32), jax.ShapeDtypeStruct((ROW, FF), F32)],
+        scratch_shapes=[pltpu.VMEM((3 * S, D), BF16), low, pltpu.VMEM((D, FF), BF16), pltpu.VMEM((FF, D), BF16), table,
+                        pltpu.VMEM((S, 1), F32)] + [table] * 5 + [low] * 9 + [pltpu.VMEM((3, S, D), BF16)] * 2
+        + [pltpu.VMEM((2, RING, S, LANES), F32), pltpu.VMEM((2, S, D), F32), pltpu.VMEM((count, S, D), F32)]
+        + [pltpu.VMEM((2, S, D), BF16)] * 2
+        + [dma((2, RING)), dma((count, RING)), dma((2,)), dma((2,)), dma((count,)), dma((2,)), dma((2,)), dma((16,))],
+        compiler_params=pltpu.CompilerParams(dimension_semantics=("arbitrary",), collective_id=1, has_side_effects=True,
+                                             vmem_limit_bytes=VMEM_LIMIT),
         cost_estimate=pl.CostEstimate(flops=count * 30_000_000_000, bytes_accessed=60_000_000, transcendentals=0),
         name="layer",
-    )(z, *args, *carried)
-
-
-def merge_kernel(firsts, half, core_ref, *refs):
-    i = pl.program_id(0)
-    for src, (own, first, count) in zip(refs[:-1], firsts):
-        at = i - first - half * jnp.where(own, core_ref[0], 1 - core_ref[0])
-
-        @pl.when((at >= 0) & (at < count))
-        def _():
-            refs[-1][...] = src[...].astype(BF16)
-
-
-def merge_call(core, owns, others):
-    counts = [v.shape[0] for v in owns]
-    half = sum(counts)
-    firsts = [(own, sum(counts[:j]), n) for own in (True, False) for j, n in enumerate(counts)]
-
-    def spec(own, first, count):
-        return pl.BlockSpec((1, S, D), lambda i, c: (
-            jnp.clip(i - first - half * (c[0] if own else 1 - c[0]), 0, count - 1), 0, 0))
-    return pl.pallas_call(
-        functools.partial(merge_kernel, firsts, half),
-        grid_spec=pltpu.PrefetchScalarGridSpec(
-            num_scalar_prefetch=1, grid=(2 * half,), in_specs=[spec(*f) for f in firsts],
-            out_specs=pl.BlockSpec((1, S, D), lambda i, c: (i, 0, 0))),
-        out_shape=jax.ShapeDtypeStruct((2 * half, S, D), BF16),
-        name="merge",
-    )(core.reshape(1).astype(jnp.int32), *owns, *others)
+    )(*args)
 
 
 STEPS, UNROLL = 8, 8
 STEP = PAD // STEPS
 
 
-def table_kernel(half, ids_ref, *refs):
-    rows, (out_ref, acc, acc2, stage, sem) = refs[:-5], refs[-5:]
-
+def table_kernel(half, ids_ref, rows_ref, out_ref, acc, acc2, stage, sem):
     @pl.loop(0, acc.shape[0] // LANES)
     def _(j):
         for a in (acc, acc2):
             a[pl.ds(pl.multiple_of(j * LANES, LANES), LANES), :] = jnp.zeros((LANES, LANES), F32)
-    start = 0
-    for even, odd in zip(rows[::2], rows[1::2]):
-        count = even.shape[0]
-
+    count = rows_ref.shape[1]
+    for k in range(0, RING, 2):
         @pl.loop(0, count // UNROLL)
-        def _(g, start=start, count=count, even=even, odd=odd):
+        def _(g):
             t0 = pl.multiple_of(g * UNROLL, UNROLL)
             for j in range(UNROLL):
-                for a, src, base in ((acc, even, start), (acc2, odd, start + count)):
-                    row = pl.ds(ids_ref[base + t0 + j], 1)
-                    a[row, :] += src[pl.ds(t0 + j, 1), :]
-        start += 2 * count
+                for a, src in ((acc, k), (acc2, k + 1)):
+                    row = pl.ds(ids_ref[src * count + t0 + j], 1)
+                    a[row, :] += rows_ref[src, pl.ds(t0 + j, 1), :]
     copies = []
     for i in range(2 * STEPS):
         h, c, slot = i // STEPS, i % STEPS, i % 2
@@ -313,14 +355,14 @@
     return pl.pallas_call(
         functools.partial(table_kernel, half),
         grid_spec=pltpu.PrefetchScalarGridSpec(
-            num_scalar_prefetch=1, grid=(), in_specs=[pl.BlockSpec(memory_space=pltpu.VMEM)] * len(rows),
+            num_scalar_prefetch=1, grid=(), in_specs=[pl.BlockSpec(memory_space=pltpu.VMEM)],
             out_specs=pl.BlockSpec(memory_space=pl.ANY),
             scratch_shapes=[pltpu.VMEM((half + PAD, LANES), F32)] * 2 + [pltpu.VMEM((2, LANES, STEP), F32), pltpu.SemaphoreType.DMA((2,))]),
         out_shape=jax.ShapeDtypeStruct((2, LANES, PAD), F32),
         compiler_params=pltpu.CompilerParams(vmem_limit_bytes=VMEM_LIMIT),
         cost_estimate=pl.CostEstimate(flops=4_000_000_000, bytes_accessed=34_000_000, transcendentals=0),
         name="table",
-    )(ids, *rows)
+    )(ids, rows)
 
 
 def cut(lo, n):
@@ -534,7 +576,6 @@
 
     def device_step(token_ids, embed_table, ln1_gain, ln1_bias, ln2_gain, ln2_bias, w_qkv, b_qkv, w_dense, b_dense, w_fc1, b_fc1, w_fc2, b_fc2, cotangent):
         core = lax.axis_index(tp)
-        z = (lax.axis_index(dp) // plane).reshape(1)
         vocab_local = embed_table.shape[0]
         seqs = token_ids.shape[0] // 2
         f = lambda v: v.astype(F32)
@@ -560,22 +601,11 @@
         x_peer = swap(f(lookup(ids_peer)))
         x_own = lookup(ids_own)
         flat = ids_own.reshape(-1)
-        ids_z = [z_shift(flat, k) for k in range(RING)]
+        ids = jnp.concatenate([z_shift(flat, k) for k in range(RING)]) - core * vocab_local
 
         args = (x_own, x_peer, cot, vec, bqkv, bfc1, rope_consts(), wq_own, wd_own, w_fc1, w_fc2, rows_peer, fc1_peer)
-        carried, owns, others, rows, row_ids, first = (), [], [], [], [], 0
-        for count in CHUNKS:
-            out, *gx_carried = layer_call(first, count, carried, z, *args)
-            gx, carried = gx_carried[:RING], gx_carried[RING:]
-            owns.append(out)
-            others.append(swap(out))
-            rows += [z_shift(gx[k], k) for k in range(RING)]
-            row_ids += [ids_z[k][first * S:(first + count) * S] for k in range(RING)]
-            first += count
-        grad_w, grad_s, grad_b1 = carried
-        layer_out = merge_call(core, owns, others)
-
-        ids = jnp.concatenate(row_ids) - core * vocab_local
+        layer_out, rows, grad_w, grad_s, grad_b1 = layer_call(*args)
+
         dense = table_call(jnp.where(ids < 0, ids + 2 * vocab_local, ids), rows, vocab_local)
 
         small = jnp.sum(grad_s, axis=1)

time: 689 us -> 564 us (0.82); the launches traced: 682 us -> 566 us
  waiting for transfers between devices: 77.7 us -> 2.6 us
  Pallas kernels: 471 us -> 445 us
  local copies, waits for them, and re-layouts: 99.2 us -> 91 us
    ppermute x9 -> x3, waiting for transfers between devices: 77.6 us -> 2.59 us  [z_shift(): lax.ppermute(v, dp, [(i, (i + k * plane) % chips) for i in range(chips)])]
    pallas_call x3 -> x1, Pallas kernels: 311 us -> 287 us  [layer_call(): pl.pallas_call(layer_kernel, grid=(count,), in_specs=[seq] * 3 + [vm] * 4...]
    unnamed x59 -> x53, local copies, waits for them, and re-layouts: 18.5 us -> 13.2 us
  transfers between devices with their start and end apart: 15 -> 7, of which waited for: 5 -> 2; matrix products, arithmetic and copies ran while one was open for 11% -> 9% of each run, Pallas kernels for 67% -> 0%
where the time goes in v2:
time: 564 us; the launch traced here: 566 us
  Pallas kernels  445 us (79%)
  local copies, waits for them, and re-layouts  91 us (16%)
  other arithmetic  19.2 us (3%)
  starting transfers between devices  7.1 us (1%)
    pallas_call x1, Pallas kernels, layer_call(): pl.pallas_call(layer_kernel, grid=(count,), in_specs=[seq] * 3 + [vm] * 4...  287 us
    pallas_call x1, Pallas kernels, tail_call(): pl.pallas_call(tail_kernel, in_specs=[hbm] * 3, out_specs=[vm] * 2, out_s...  98.6 us
    pallas_call x1, Pallas kernels, table_call(): pl.pallas_call(functools.partial(table_kernel, half), grid_spec=pltpu.Pre...  58.6 us
    gather x2, local copies, waits for them, and re-layouts, lookup(): got = jnp.take(embed_table, jnp.where(ok, local, 0), axis=0)  58.2 us
    unnamed x53, local copies, waits for them, and re-layouts  13.2 us
  transfers between devices with their start and end apart: 7, of which 2 were waited for; matrix products, arithmetic and copies ran while one was open for 9% of the time, Pallas kernels for 0%

profile of v2, /device:TPU:0, one launch (start us, length us, event | category | flops | bytes accessed | tf_op | source)
XLA Modules:
  0.0 566.0 jit_solution(17867209203290135544)
XLA Ops:
  0.7 0.8 compare_and_fusion
  1.4 0.8 dynamic-slice_bitcast_fusion
  2.2 29.0 %gather_fusion.1 = bf16[4096,512]{1,0:T(8,128)(2,1)} fusion(bf16[25152,512]{1,0:T(8,128)(2,1)} %param.18, s32[4096]{0:T(1024)S(1)} %get-tuple-element.48), kind=kCustom, calls=%fused_computation.1.clone | custom fusion | bytes 8404992 | tf_op jit(solution)/shard_map/jit(_take)/gather | solution.py:595
  31.3 7.1 %fusion = f32[8,512,512]{2,1,0:T(8,128)} fusion(bf16[8,512,512]{2,1,0:T(8,128)(2,1)} %bitcast.62, pred[8,512]{1,0:T(8,128)(4,1)S(1)} %get-tuple-element.29, pred[8,512]{1,0:T(8,128)(4,1)S(1)} %get-tuple-element.30), kind=kLoop, calls=%fused_computation.3 | loop fusion | flops 6291456 | bytes 12591104 | tf_op jit(solution)/shard_map/convert_element_type | solution.py:581
  38.3 0.1 collective-permute-start
  38.4 0.1 copy.43
  38.5 0.9 copy-done.1
  39.4 2.5 maximum_convert_fusion
  41.9 0.5 collective-permute-start.2
  42.4 0.1 reshape.104
  42.5 0.1 collective-permute-start.1
  42.6 0.2 convert_element_type.37
  42.9 0.6 collective-permute-start.3
  43.4 4.5 collective-permute-start.6
  48.0 29.1 %gather_fusion = bf16[4096,512]{1,0:T(8,128)(2,1)} fusion(bf16[25152,512]{1,0:T(8,128)(2,1)} %param.18, s32[4096]{0:T(1024)S(1)} %get-tuple-element.49), kind=kCustom, calls=%fused_computation.clone | custom fusion | bytes 8404992 | tf_op jit(solution)/shard_map/jit(_take)/gather | solution.py:595
  77.1 1.0 fusion.1
  78.1 1.1 concatenate.36
  79.3 1.1 concatenate.35
  80.4 1.1 concatenate.34
  81.5 0.4 concatenate.33
  82.0 1.0 bitcast_dynamic-update-slice_fusion.2
  82.9 1.0 bitcast_dynamic-update-slice_fusion.1
  84.0 0.0 copy-start.17
  84.0 0.0 copy-start.18
  84.0 4.6 constant_dynamic-slice_fusion.cot_ref
  88.6 0.0 copy-start.8
  88.6 0.0 copy-start.13
  88.7 0.0 copy-start.14
  88.7 3.7 select_select_fusion.1.xo_ref
  92.5 1.2 copy-done.10
  93.7 0.6 stack.57.vec_ref
  94.4 0.1 reshape.105
  94.5 1.3 collective-permute-start.4
  95.8 0.6 pad_maximum_fusion
  96.4 0.7 reshape.106.bqkv_ref
  97.1 2.5 collective-permute-done.5
  99.6 0.1 collective-permute-done.4
  99.7 0.6 compare_select_fusion.ids_ref
  100.3 287.5 %layer.1 = (bf16[16,512,512]{2,1,0:T(8,128)(2,1)}, f32[4,4096,128]{2,1,0:T(8,128)}, f32[512,6144]{1,0:T(8,128)}, f32[8,8,512]{2,1,0:T(8,128)}, f32[8,2048]{1,0:T(8,128)}) custom-call(bf16[8,512,512]{2,1,0:T(8,128)(2,1)} %select_select_fusion.1.xo_ref, f32[8,512,512]{2,1,0:T(8,128)} %collective-permute-done.xp_ref, ...), custom_call_target="tpu_custom_call" | custom-call | flops 240000008192 | bytes 60000000 | tf_op jit(solution)/shard_map/layer/pallas_call | solution.py:301
  387.8 0.9 reduce_sum.19
  388.7 0.1 reshape.116
  388.8 0.1 copy.47
  388.8 0.9 reduce_sum.18
  389.8 0.1 reshape.114
  389.9 0.1 reshape.115
  390.0 0.1 copy.46
  390.1 0.1 reshape.113
  390.2 0.1 copy.44
  390.3 0.1 copy.50
  390.4 0.8 pad.4.clone
  391.3 58.6 %table.1 = f32[2,128,25600]{2,1,0:T(8,128)} custom-call(s32[16384]{0:T(1024)} %compare_select_fusion.ids_ref, f32[4,4096,128]{2,1,0:T(8,128)} %get-tuple-element.23.rows_ref), custom_call_target="tpu_custom_call" | custom-call | flops 4000000000 | bytes 34000000 | tf_op jit(solution)/shard_map/table/pallas_call | solution.py:355
  449.9 98.6 %tail.1 = (f32[8,25152]{1,0:T(8,128)}, f32[8,3200]{1,0:T(8,128)}) custom-call(f32[2,4,4,8,25600]{4,3,2,1,0:T(8,128)} %bitcast.60, f32[4,4,4,8,6144]{4,3,2,1,0:T(8,128)} %bitcast.63, f32[2,4,4,4,8,128]{5,4,3,2,1,0:T(8,128)} %bitcast.66), custom_call_target="tpu_custom_call" | custom-call | tf_op jit(solution)/shard_map/tail/pallas_call | solution.py:552
  548.5 1.5 slice_bitcast_fusion.2
  550.0 0.7 slice.56
  550.8 1.3 slice_bitcast_fusion.3
  552.0 0.7 slice.59
  552.7 1.4 slice_bitcast_fusion
  554.1 1.3 slice_bitcast_fusion.1
  555.4 0.7 reshape.118
  556.1 0.1 reshape.119
  556.2 0.6 copy.55
  556.8 0.5 copy.64
  557.3 7.6 %copy.65 = bf16[16,512,512]{2,1,0:T(8,128)(2,1)} copy(bf16[16,512,512]{2,1,0:T(8,128)(2,1)} %get-tuple-element.92) | data formatting | bytes 16777216
  564.9 0.9 copy.66
  (67 shorter events, 0.4 us)
Async XLA Ops:
  31.3 7.2 %copy-start.6 = (bf16[512,4,3,64]{0,3,2,1:T(8,128)(2,1)S(1)}, bf16[512,4,3,64]{0,3,2,1:T(8,128)(2,1)}, u32[]{:S(2)}) copy-start(bf16[512,4,3,64]{0,3,2,1:T(8,128)(2,1)} %param.23) | copy-start | bytes 2359300
  31.3 8.1 %copy-start.4 = (bf16[1024,512]{1,0:T(8,128)(2,1)S(1)}, bf16[1024,512]{1,0:T(8,128)(2,1)}, u32[]{:S(2)}) copy-start(bf16[1024,512]{1,0:T(8,128)(2,1)} %to_ref.1) | copy-start | bytes 3145732
  31.3 8.1 %copy-start.7 = (bf16[4,64,512]{2,1,0:T(8,128)(2,1)S(1)}, bf16[4,64,512]{2,1,0:T(8,128)(2,1)}, u32[]{:S(2)}) copy-start(bf16[4,64,512]{2,1,0:T(8,128)(2,1)} %param.25) | copy-start | bytes 786436
  38.3 4.1 copy-start.11
  38.3 4.2 copy-start.12
  38.3 4.3 copy-start.2
  38.3 62.0 %collective-permute-start = (f32[8,512,512]{2,1,0:T(8,128)}, f32[8,512,512]{2,1,0:T(8,128)}, u32[]{:S(2)}, u32[]{:S(2)}) collective-permute-start(f32[8,512,512]{2,1,0:T(8,128)} %fusion), channel_id=1, source_target_pairs={{0,64},{64,0},{1,65},{65,1},{2,66},{66,2},{3,67},{67,3},{4,68},{68... | collective-permute-start | bytes 25165832 | tf_op jit(solution)/shard_map/ppermute | solution.py:572
  38.5 0.9 copy-start.1
  41.9 58.4 %collective-permute-start.2 = (f32[2048,512]{1,0:T(8,128)}, f32[2048,512]{1,0:T(8,128)}, u32[]{:S(2)}, u32[]{:S(2)}) collective-permute-start(f32[2048,512]{1,0:T(8,128)} %maximum_convert_fusion), channel_id=1, source_target_pairs={{0,64},{64,0},{1,65},{65,1},{2,66},{66,2},{3,67},{67,3},{4,68},{68... | collective-permute-start | bytes 12582920 | tf_op jit(solution)/shard_map/ppermute | solution.py:572
  42.5 51.8 %collective-permute-start.1 = (f32[1792]{0:T(1024)S(1)}, f32[1792]{0:T(1024)S(1)}, u32[]{:S(2)}, u32[]{:S(2)}) collective-permute-start(f32[1792]{0:T(1024)S(1)} %maximum_convert_fusion.1), channel_id=1, source_target_pairs={{0,64},{64,0},{1,65},{65,1},{2,66},{66,2},{3,67},{67,3},{4,68},{68... | collective-permute-start | bytes 21512 | tf_op jit(solution)/shard_map/ppermute | solution.py:572
  42.9 57.5 %collective-permute-start.3 = (f32[512,1024]{1,0:T(8,128)S(1)}, f32[512,1024]{1,0:T(8,128)}, u32[]{:S(2)}, u32[]{:S(2)}) collective-permute-start(f32[512,1024]{1,0:T(8,128)S(1)} %convert_element_type.37), channel_id=1, source_target_pairs={{0,64},{64,0},{1,65},{65,1},{2,66},{66,2},{3,67},{67,3},{4,68},{68... | collective-permute-start | bytes 6291464 | tf_op jit(solution)/shard_map/ppermute | solution.py:572
  43.4 51.0 %collective-permute-start.6 = (s32[4096]{0:T(1024)S(1)}, s32[4096]{0:T(1024)S(1)}, u32[]{:S(2)}, u32[]{:S(2)}) collective-permute-start(s32[4096]{0:T(1024)S(1)} %bitcast.76), channel_id=1, source_target_pairs={{0,48},{1,49},{2,50},{3,51},{4,52},{5,53},{6,54},{7,55},{8,56},{9,... | collective-permute-start | bytes 49160 | tf_op jit(solution)/shard_map/ppermute | solution.py:575
  80.4 3.6 copy-start.3
  81.5 2.5 copy-start.9
  84.0 4.6 copy-start.17
  84.0 4.6 copy-start.18
  84.0 4.6 copy-start
  88.6 3.8 copy-start.8
  88.6 5.0 copy-start.13
  88.7 5.0 copy-start.14
  88.7 5.0 copy-start.15
  88.7 5.0 copy-start.16
  92.5 1.2 copy-start.10
  94.4 5.2 collective-permute-start.5
  94.5 5.2 collective-permute-start.4
  550.0 14.9 %copy-start.19 = (f32[8]{0:T(128)}, f32[8]{0:T(128)S(1)}, u32[]{:S(2)}) copy-start(f32[8]{0:T(128)S(1)} %get-tuple-element.101) | copy-start | bytes 100
  557.3 7.6 %copy-start.5 = (f32[8,25152]{1,0:T(8,128)S(1)}, f32[8,25152]{1,0:T(8,128)}, u32[]{:S(2)}) copy-start(f32[8,25152]{1,0:T(8,128)} %get-tuple-element.27) | copy-start | bytes 2414596
